TPU v7x, 32 devices: a 4x4x1 block of a 4x4x8 slice. The times are simulated.
32 devices in a mesh: dp: 1 (over z), tp: 4 (over y), pp: 8 (over x, core).
Axes of the slice: x: 4, y: 4, z: 1, core: 2. Of those that a mesh axis runs over, the one named last changes fastest.
The devices are a block of a 4x4x8 slice.
Arguments:
- x_in: bfloat16 [4, 1, 1024, 1024], P('dp')
- seq_lens: int32 [4, 1], P('dp')
- ln1_gain: bfloat16 [8, 1024], P('pp')
- ln1_shift: bfloat16 [8, 1024], P('pp')
- w_qkv: bfloat16 [8, 1024, 3, 1024], P('pp', None, None, 'tp')
- b_qkv: bfloat16 [8, 3, 16, 64], P('pp', None, 'tp')
- w_out: bfloat16 [8, 1024, 1024], P('pp', 'tp')
- b_out: bfloat16 [8, 1024], P('pp')
- ln2_gain: bfloat16 [8, 1024], P('pp')
- ln2_shift: bfloat16 [8, 1024], P('pp')
- w_up: bfloat16 [8, 1024, 4096], P('pp', None, 'tp')
- b_up: bfloat16 [8, 4096], P('pp', 'tp')
- w_down: bfloat16 [8, 4096, 1024], P('pp', 'tp')
- b_down: bfloat16 [8, 1024], P('pp')
Outputs:
- output: bfloat16 [8, 4, 1, 1024, 1024], P('pp', 'dp')
All inputs are finite; a program needn't handle non-finite values.
Results may differ from a plain program's by a relative error of at most 0.02.
Values are sent between devices in bfloat16 or wider.
A program may use at most 768 MiB of HBM per device.

v0:
```python
import jax
import jax.numpy as jnp
from jax import lax
from jax.sharding import PartitionSpec as P
import math


def alibi_slopes(heads_n):
    closest = 2 ** int(math.floor(math.log2(heads_n)))
    base_rate = 2.0 ** (-8.0 / closest)
    slope_list = [base_rate ** (head_idx + 1) for head_idx in range(closest)]
    extra_rate = 2.0 ** (-4.0 / closest)
    slope_list = slope_list + [extra_rate ** (2 * head_idx + 1) for head_idx in range(min(closest, heads_n - closest))]
    return jnp.array(slope_list, dtype=jnp.float32)


def layer_norm(values, gain_vec, shift_vec):
    val_f = values.astype(jnp.float32)
    mean_val = jnp.mean(val_f, axis=-1, keepdims=True)
    centered = val_f - mean_val
    var_val = jnp.mean(centered * centered, axis=-1, keepdims=True)
    normed = centered * lax.rsqrt(var_val + 1e-5)
    return (normed * gain_vec.astype(jnp.float32) + shift_vec.astype(jnp.float32)).astype(jnp.bfloat16)


def attention(query_all, key_all, val_all, slopes, lens_row):
    batch_n, seq_n, heads_n, head_dim = query_all.shape
    blk_len = min(seq_n, 128)
    key_pos = jnp.arange(seq_n)
    key_ok = key_pos[None, :] < lens_row[:, None]

    def one_block(blk_idx):
        query_blk = lax.dynamic_slice_in_dim(query_all, blk_idx * blk_len, blk_len, 1)
        scores = jnp.einsum('bqhe,bkhe->bhqk', query_blk, key_all, preferred_element_type=jnp.float32) * (head_dim ** -0.5)
        query_pos = blk_idx * blk_len + jnp.arange(blk_len)
        distance = (query_pos[:, None] - key_pos[None, :]).astype(jnp.float32)
        scores = scores - slopes[None, :, None, None] * distance[None, None]
        allowed = (key_pos[None, :] <= query_pos[:, None])[None, None] & key_ok[:, None, None, :]
        scores = jnp.where(allowed, scores, -1e30)
        prob_bf = jax.nn.softmax(scores, axis=-1).astype(jnp.bfloat16)
        return jnp.einsum('bhqk,bkhe->bqhe', prob_bf, val_all, preferred_element_type=jnp.float32).astype(jnp.bfloat16)

    return lax.map(one_block, jnp.arange(seq_n // blk_len))


def stage_layer(act_in, lens_row, layer_w, slopes):
    ln1_gain, ln1_shift, w_qkv, b_qkv, w_out, b_out, ln2_gain, ln2_shift, w_up, b_up, w_down, b_down = layer_w
    batch_n, seq_n, model_n = act_in.shape
    tokens_n = batch_n * seq_n
    heads_loc, head_dim = b_qkv.shape[1], b_qkv.shape[2]
    width_loc = heads_loc * head_dim
    flat_in = act_in.reshape(tokens_n, model_n)
    normed = layer_norm(flat_in, ln1_gain, ln1_shift)
    qkv_loc = (jnp.dot(normed, w_qkv.reshape(model_n, 3 * width_loc), preferred_element_type=jnp.float32) + b_qkv.reshape(3 * width_loc).astype(jnp.float32)).astype(jnp.bfloat16)
    qkv_loc = qkv_loc.reshape(batch_n, seq_n, 3, heads_loc, head_dim)
    ctx_blocks = attention(qkv_loc[:, :, 0], qkv_loc[:, :, 1], qkv_loc[:, :, 2], slopes, lens_row)
    attn_part = jnp.einsum('nbqhe,hef->bnqf', ctx_blocks, w_out.reshape(heads_loc, head_dim, model_n), preferred_element_type=jnp.float32).astype(jnp.bfloat16)
    attn_sum = lax.psum(attn_part.reshape(tokens_n, model_n), 'tp')
    resid_act = (flat_in.astype(jnp.float32) + attn_sum.astype(jnp.float32) + b_out.astype(jnp.float32)).astype(jnp.bfloat16)
    normed_mlp = layer_norm(resid_act, ln2_gain, ln2_shift)
    hidden_act = jax.nn.gelu(jnp.dot(normed_mlp, w_up, preferred_element_type=jnp.float32) + b_up.astype(jnp.float32), approximate=True).astype(jnp.bfloat16)
    mlp_part = jnp.dot(hidden_act, w_down, preferred_element_type=jnp.float32).astype(jnp.bfloat16)
    mlp_sum = lax.psum(mlp_part, 'tp')
    result = (resid_act.astype(jnp.float32) + mlp_sum.astype(jnp.float32) + b_down.astype(jnp.float32)).astype(jnp.bfloat16)
    return result.reshape(batch_n, seq_n, model_n)


def solution(mesh):
    stages = mesh.shape['pp']
    tp_size = mesh.shape['tp']
    next_pairs = [(src_stage, src_stage + 1) for src_stage in range(stages - 1)]
    in_specs = (P('dp'), P('dp'), P('pp'), P('pp'), P('pp', None, None, 'tp'), P('pp', None, 'tp', None), P('pp', 'tp', None), P('pp'), P('pp'), P('pp'), P('pp', None, 'tp'), P('pp', 'tp'), P('pp', 'tp', None), P('pp'))

    def per_device(x_in, seq_lens, ln1_gain, ln1_shift, w_qkv, b_qkv, w_out, b_out, ln2_gain, ln2_shift, w_up, b_up, w_down, b_down):
        stage_idx = lax.axis_index('pp')
        tp_rank = lax.axis_index('tp')
        layer_w = tuple(stacked[0] for stacked in (ln1_gain, ln1_shift, w_qkv, b_qkv, w_out, b_out, ln2_gain, ln2_shift, w_up, b_up, w_down, b_down))
        heads_loc = b_qkv.shape[2]
        slopes = lax.dynamic_slice_in_dim(alibi_slopes(heads_loc * tp_size), tp_rank * heads_loc, heads_loc)
        micro_n = x_in.shape[0]

        def one_step(time_idx, loop_state):
            received, outputs = loop_state
            first_in = lax.dynamic_index_in_dim(x_in, jnp.minimum(time_idx, micro_n - 1), 0, keepdims=False)
            act_in = jnp.where(stage_idx == 0, first_in, received)
            micro_idx = jnp.clip(time_idx - stage_idx, 0, micro_n - 1)
            lens_row = lax.dynamic_index_in_dim(seq_lens, micro_idx, 0, keepdims=False)
            act_out = stage_layer(act_in, lens_row, layer_w, slopes)
            active = (time_idx >= stage_idx) & (time_idx - stage_idx < micro_n)
            previous = lax.dynamic_index_in_dim(outputs, micro_idx, 0, keepdims=False)
            outputs = lax.dynamic_update_index_in_dim(outputs, jnp.where(active, act_out, previous), micro_idx, 0)
            received = lax.ppermute(act_out, 'pp', next_pairs)
            return received, outputs

        loop_init = (jnp.zeros(x_in.shape[1:], x_in.dtype), jnp.zeros(x_in.shape, x_in.dtype))
        last_recv, outputs = lax.fori_loop(0, micro_n + stages - 1, one_step, loop_init)
        return outputs[None]

    return jax.shard_map(per_device, mesh=mesh, in_specs=in_specs, out_specs=P('pp', 'dp'), check_vma=False)
```

profile of v0, /device:TPU:103, one launch (start us, length us, event | category | flops | bytes accessed | tf_op | source)
XLA Modules:
  0.0 2421.0 jit_solution(14130899067003721860)
XLA Ops:
  16.3 2397.8 %while.44 = (s32[]{:T(128)}, bf16[1,1024,1024]{2,1,0:T(8,128)(2,1)}, bf16[4,1,1024,1024]{3,2,1,0:T(8,128)(2,1)}, pred[]{:T(512)}, bf16[4,1,1024,1024]{3,2,1,0:T(...) while((s32[]{:T(128)}, ...), condition=%wide.region_11.12_spmd, body=%wide.region_0.11_spmd.sunk | while | flops 6640675840 | bytes 112757608 | solution.py:96
  24.3 58.4 %while.45 = (s32[]{:T(128)}, bf16[8,1,128,4,64]{2,4,3,1,0:T(8,128)(2,1)}, s32[8]{0:T(128)S(1)}, bf16[1,1024,4,64]{1,3,2,0:T(8,128)(2,1)S(1)}, bf16[1,1024,4,64]{...) while((s32[]{:T(128)}, ...), condition=%wide.region_6.6_spmd.clone.clone, body=%wide.region_3.5_spmd.clone.clone.sunk | while | flops 138971264 | bytes 6693563 | solution.py:43
  86.0 55.9 %all-reduce.3.cloned.1.call-done = bf16[1024,1024]{1,0:T(8,128)(2,1)} async-done(((bf16[1024,1024]{1,0:T(8,128)(2,1)}), bf16[1024,1024]{1,0:T(8,128)(2,1)}) %all-reduce.3.cloned.1.call-update) | async-done | bytes 2097168 | tf_op jit(solution)/shard_map/while/body/eval_jaxpr/psum | solution.py:58
  225.7 58.4 %while.45 = (s32[]{:T(128)}, bf16[8,1,128,4,64]{2,4,3,1,0:T(8,128)(2,1)}, s32[8]{0:T(128)S(1)}, bf16[1,1024,4,64]{1,3,2,0:T(8,128)(2,1)S(1)}, bf16[1,1024,4,64]{...) while((s32[]{:T(128)}, ...), condition=%wide.region_6.6_spmd.clone.clone, body=%wide.region_3.5_spmd.clone.clone.sunk | while | flops 138971264 | bytes 6693563 | solution.py:43
  287.4 74.1 %all-reduce.3.cloned.1.call-done = bf16[1024,1024]{1,0:T(8,128)(2,1)} async-done(((bf16[1024,1024]{1,0:T(8,128)(2,1)}), bf16[1024,1024]{1,0:T(8,128)(2,1)}) %all-reduce.3.cloned.1.call-update) | async-done | bytes 2097168 | tf_op jit(solution)/shard_map/while/body/eval_jaxpr/psum | solution.py:58
  373.7 53.3 %all-reduce.5.cloned.1.call-done = bf16[1024,1024]{1,0:T(8,128)(2,1)} async-done(((bf16[1024,1024]{1,0:T(8,128)(2,1)}), bf16[1024,1024]{1,0:T(8,128)(2,1)}) %all-reduce.5.cloned.1.call-update) | async-done | bytes 2097168 | tf_op jit(solution)/shard_map/while/body/eval_jaxpr/psum | solution.py:63
  445.3 58.4 %while.45 = (s32[]{:T(128)}, bf16[8,1,128,4,64]{2,4,3,1,0:T(8,128)(2,1)}, s32[8]{0:T(128)S(1)}, bf16[1,1024,4,64]{1,3,2,0:T(8,128)(2,1)S(1)}, bf16[1,1024,4,64]{...) while((s32[]{:T(128)}, ...), condition=%wide.region_6.6_spmd.clone.clone, body=%wide.region_3.5_spmd.clone.clone.sunk | while | flops 138971264 | bytes 6693563 | solution.py:43
  507.0 74.1 %all-reduce.3.cloned.1.call-done = bf16[1024,1024]{1,0:T(8,128)(2,1)} async-done(((bf16[1024,1024]{1,0:T(8,128)(2,1)}), bf16[1024,1024]{1,0:T(8,128)(2,1)}) %all-reduce.3.cloned.1.call-update) | async-done | bytes 2097168 | tf_op jit(solution)/shard_map/while/body/eval_jaxpr/psum | solution.py:58
  593.4 53.3 %all-reduce.5.cloned.1.call-done = bf16[1024,1024]{1,0:T(8,128)(2,1)} async-done(((bf16[1024,1024]{1,0:T(8,128)(2,1)}), bf16[1024,1024]{1,0:T(8,128)(2,1)}) %all-reduce.5.cloned.1.call-update) | async-done | bytes 2097168 | tf_op jit(solution)/shard_map/while/body/eval_jaxpr/psum | solution.py:63
  665.0 58.4 %while.45 = (s32[]{:T(128)}, bf16[8,1,128,4,64]{2,4,3,1,0:T(8,128)(2,1)}, s32[8]{0:T(128)S(1)}, bf16[1,1024,4,64]{1,3,2,0:T(8,128)(2,1)S(1)}, bf16[1,1024,4,64]{...) while((s32[]{:T(128)}, ...), condition=%wide.region_6.6_spmd.clone.clone, body=%wide.region_3.5_spmd.clone.clone.sunk | while | flops 138971264 | bytes 6693563 | solution.py:43
  726.6 74.1 %all-reduce.3.cloned.1.call-done = bf16[1024,1024]{1,0:T(8,128)(2,1)} async-done(((bf16[1024,1024]{1,0:T(8,128)(2,1)}), bf16[1024,1024]{1,0:T(8,128)(2,1)}) %all-reduce.3.cloned.1.call-update) | async-done | bytes 2097168 | tf_op jit(solution)/shard_map/while/body/eval_jaxpr/psum | solution.py:58
  813.0 53.3 %all-reduce.5.cloned.1.call-done = bf16[1024,1024]{1,0:T(8,128)(2,1)} async-done(((bf16[1024,1024]{1,0:T(8,128)(2,1)}), bf16[1024,1024]{1,0:T(8,128)(2,1)}) %all-reduce.5.cloned.1.call-update) | async-done | bytes 2097168 | tf_op jit(solution)/shard_map/while/body/eval_jaxpr/psum | solution.py:63
  884.6 58.4 %while.45 = (s32[]{:T(128)}, bf16[8,1,128,4,64]{2,4,3,1,0:T(8,128)(2,1)}, s32[8]{0:T(128)S(1)}, bf16[1,1024,4,64]{1,3,2,0:T(8,128)(2,1)S(1)}, bf16[1,1024,4,64]{...) while((s32[]{:T(128)}, ...), condition=%wide.region_6.6_spmd.clone.clone, body=%wide.region_3.5_spmd.clone.clone.sunk | while | flops 138971264 | bytes 6693563 | solution.py:43
  946.3 74.1 %all-reduce.3.cloned.1.call-done = bf16[1024,1024]{1,0:T(8,128)(2,1)} async-done(((bf16[1024,1024]{1,0:T(8,128)(2,1)}), bf16[1024,1024]{1,0:T(8,128)(2,1)}) %all-reduce.3.cloned.1.call-update) | async-done | bytes 2097168 | tf_op jit(solution)/shard_map/while/body/eval_jaxpr/psum | solution.py:58
  1032.7 53.3 %all-reduce.5.cloned.1.call-done = bf16[1024,1024]{1,0:T(8,128)(2,1)} async-done(((bf16[1024,1024]{1,0:T(8,128)(2,1)}), bf16[1024,1024]{1,0:T(8,128)(2,1)}) %all-reduce.5.cloned.1.call-update) | async-done | bytes 2097168 | tf_op jit(solution)/shard_map/while/body/eval_jaxpr/psum | solution.py:63
  1104.2 58.4 %while.45 = (s32[]{:T(128)}, bf16[8,1,128,4,64]{2,4,3,1,0:T(8,128)(2,1)}, s32[8]{0:T(128)S(1)}, bf16[1,1024,4,64]{1,3,2,0:T(8,128)(2,1)S(1)}, bf16[1,1024,4,64]{...) while((s32[]{:T(128)}, ...), condition=%wide.region_6.6_spmd.clone.clone, body=%wide.region_3.5_spmd.clone.clone.sunk | while | flops 138971264 | bytes 6693563 | solution.py:43
  1165.9 74.1 %all-reduce.3.cloned.1.call-done = bf16[1024,1024]{1,0:T(8,128)(2,1)} async-done(((bf16[1024,1024]{1,0:T(8,128)(2,1)}), bf16[1024,1024]{1,0:T(8,128)(2,1)}) %all-reduce.3.cloned.1.call-update) | async-done | bytes 2097168 | tf_op jit(solution)/shard_map/while/body/eval_jaxpr/psum | solution.py:58
  1252.3 53.3 %all-reduce.5.cloned.1.call-done = bf16[1024,1024]{1,0:T(8,128)(2,1)} async-done(((bf16[1024,1024]{1,0:T(8,128)(2,1)}), bf16[1024,1024]{1,0:T(8,128)(2,1)}) %all-reduce.5.cloned.1.call-update) | async-done | bytes 2097168 | tf_op jit(solution)/shard_map/while/body/eval_jaxpr/psum | solution.py:63
  1323.9 58.4 %while.45 = (s32[]{:T(128)}, bf16[8,1,128,4,64]{2,4,3,1,0:T(8,128)(2,1)}, s32[8]{0:T(128)S(1)}, bf16[1,1024,4,64]{1,3,2,0:T(8,128)(2,1)S(1)}, bf16[1,1024,4,64]{...) while((s32[]{:T(128)}, ...), condition=%wide.region_6.6_spmd.clone.clone, body=%wide.region_3.5_spmd.clone.clone.sunk | while | flops 138971264 | bytes 6693563 | solution.py:43
  1385.5 74.1 %all-reduce.3.cloned.1.call-done = bf16[1024,1024]{1,0:T(8,128)(2,1)} async-done(((bf16[1024,1024]{1,0:T(8,128)(2,1)}), bf16[1024,1024]{1,0:T(8,128)(2,1)}) %all-reduce.3.cloned.1.call-update) | async-done | bytes 2097168 | tf_op jit(solution)/shard_map/while/body/eval_jaxpr/psum | solution.py:58
  1471.9 53.3 %all-reduce.5.cloned.1.call-done = bf16[1024,1024]{1,0:T(8,128)(2,1)} async-done(((bf16[1024,1024]{1,0:T(8,128)(2,1)}), bf16[1024,1024]{1,0:T(8,128)(2,1)}) %all-reduce.5.cloned.1.call-update) | async-done | bytes 2097168 | tf_op jit(solution)/shard_map/while/body/eval_jaxpr/psum | solution.py:63
  1543.5 58.4 %while.45 = (s32[]{:T(128)}, bf16[8,1,128,4,64]{2,4,3,1,0:T(8,128)(2,1)}, s32[8]{0:T(128)S(1)}, bf16[1,1024,4,64]{1,3,2,0:T(8,128)(2,1)S(1)}, bf16[1,1024,4,64]{...) while((s32[]{:T(128)}, ...), condition=%wide.region_6.6_spmd.clone.clone, body=%wide.region_3.5_spmd.clone.clone.sunk | while | flops 138971264 | bytes 6693563 | solution.py:43
  1605.2 74.1 %all-reduce.3.cloned.1.call-done = bf16[1024,1024]{1,0:T(8,128)(2,1)} async-done(((bf16[1024,1024]{1,0:T(8,128)(2,1)}), bf16[1024,1024]{1,0:T(8,128)(2,1)}) %all-reduce.3.cloned.1.call-update) | async-done | bytes 2097168 | tf_op jit(solution)/shard_map/while/body/eval_jaxpr/psum | solution.py:58
  1691.6 53.3 %all-reduce.5.cloned.1.call-done = bf16[1024,1024]{1,0:T(8,128)(2,1)} async-done(((bf16[1024,1024]{1,0:T(8,128)(2,1)}), bf16[1024,1024]{1,0:T(8,128)(2,1)}) %all-reduce.5.cloned.1.call-update) | async-done | bytes 2097168 | tf_op jit(solution)/shard_map/while/body/eval_jaxpr/psum | solution.py:63
  1763.2 58.4 %while.45 = (s32[]{:T(128)}, bf16[8,1,128,4,64]{2,4,3,1,0:T(8,128)(2,1)}, s32[8]{0:T(128)S(1)}, bf16[1,1024,4,64]{1,3,2,0:T(8,128)(2,1)S(1)}, bf16[1,1024,4,64]{...) while((s32[]{:T(128)}, ...), condition=%wide.region_6.6_spmd.clone.clone, body=%wide.region_3.5_spmd.clone.clone.sunk | while | flops 138971264 | bytes 6693563 | solution.py:43
  1824.8 74.1 %all-reduce.3.cloned.1.call-done = bf16[1024,1024]{1,0:T(8,128)(2,1)} async-done(((bf16[1024,1024]{1,0:T(8,128)(2,1)}), bf16[1024,1024]{1,0:T(8,128)(2,1)}) %all-reduce.3.cloned.1.call-update) | async-done | bytes 2097168 | tf_op jit(solution)/shard_map/while/body/eval_jaxpr/psum | solution.py:58
  1911.2 53.3 %all-reduce.5.cloned.1.call-done = bf16[1024,1024]{1,0:T(8,128)(2,1)} async-done(((bf16[1024,1024]{1,0:T(8,128)(2,1)}), bf16[1024,1024]{1,0:T(8,128)(2,1)}) %all-reduce.5.cloned.1.call-update) | async-done | bytes 2097168 | tf_op jit(solution)/shard_map/while/body/eval_jaxpr/psum | solution.py:63
  1982.8 58.4 %while.45 = (s32[]{:T(128)}, bf16[8,1,128,4,64]{2,4,3,1,0:T(8,128)(2,1)}, s32[8]{0:T(128)S(1)}, bf16[1,1024,4,64]{1,3,2,0:T(8,128)(2,1)S(1)}, bf16[1,1024,4,64]{...) while((s32[]{:T(128)}, ...), condition=%wide.region_6.6_spmd.clone.clone, body=%wide.region_3.5_spmd.clone.clone.sunk | while | flops 138971264 | bytes 6693563 | solution.py:43
  2044.5 74.1 %all-reduce.3.cloned.1.call-done = bf16[1024,1024]{1,0:T(8,128)(2,1)} async-done(((bf16[1024,1024]{1,0:T(8,128)(2,1)}), bf16[1024,1024]{1,0:T(8,128)(2,1)}) %all-reduce.3.cloned.1.call-update) | async-done | bytes 2097168 | tf_op jit(solution)/shard_map/while/body/eval_jaxpr/psum | solution.py:58
  2130.9 53.3 %all-reduce.5.cloned.1.call-done = bf16[1024,1024]{1,0:T(8,128)(2,1)} async-done(((bf16[1024,1024]{1,0:T(8,128)(2,1)}), bf16[1024,1024]{1,0:T(8,128)(2,1)}) %all-reduce.5.cloned.1.call-update) | async-done | bytes 2097168 | tf_op jit(solution)/shard_map/while/body/eval_jaxpr/psum | solution.py:63
  2202.4 58.4 %while.45 = (s32[]{:T(128)}, bf16[8,1,128,4,64]{2,4,3,1,0:T(8,128)(2,1)}, s32[8]{0:T(128)S(1)}, bf16[1,1024,4,64]{1,3,2,0:T(8,128)(2,1)S(1)}, bf16[1,1024,4,64]{...) while((s32[]{:T(128)}, ...), condition=%wide.region_6.6_spmd.clone.clone, body=%wide.region_3.5_spmd.clone.clone.sunk | while | flops 138971264 | bytes 6693563 | solution.py:43
  2264.1 74.1 %all-reduce.3.cloned.1.call-done = bf16[1024,1024]{1,0:T(8,128)(2,1)} async-done(((bf16[1024,1024]{1,0:T(8,128)(2,1)}), bf16[1024,1024]{1,0:T(8,128)(2,1)}) %all-reduce.3.cloned.1.call-update) | async-done | bytes 2097168 | tf_op jit(solution)/shard_map/while/body/eval_jaxpr/psum | solution.py:58
  (1045 shorter events, 1065.5 us)
Async XLA Ops:
  16.3 125.5 %all-reduce.3.cloned.1.call-start = ((), (), s32[]{:S(2)}) async-start(), calls=%async_computation | async-start | bytes 4194304 | tf_op jit(solution)/shard_map/while/body/eval_jaxpr/psum | solution.py:58
  85.9 121.6 %all-reduce.5.cloned.1.call-start = ((), (), s32[]{:S(2)}) async-start(), calls=%async_computation.1 | async-start | bytes 4194304 | tf_op jit(solution)/shard_map/while/body/eval_jaxpr/psum | solution.py:63
  211.3 6.4 collective-permute-start
  217.8 143.7 %all-reduce.3.cloned.1.call-start = ((), (), s32[]{:S(2)}) async-start(), calls=%async_computation | async-start | bytes 4194304 | tf_op jit(solution)/shard_map/while/body/eval_jaxpr/psum | solution.py:58
  287.2 139.8 %all-reduce.5.cloned.1.call-start = ((), (), s32[]{:S(2)}) async-start(), calls=%async_computation.1 | async-start | bytes 4194304 | tf_op jit(solution)/shard_map/while/body/eval_jaxpr/psum | solution.py:63
  431.0 6.4 collective-permute-start
  437.4 143.7 %all-reduce.3.cloned.1.call-start = ((), (), s32[]{:S(2)}) async-start(), calls=%async_computation | async-start | bytes 4194304 | tf_op jit(solution)/shard_map/while/body/eval_jaxpr/psum | solution.py:58
  506.9 139.8 %all-reduce.5.cloned.1.call-start = ((), (), s32[]{:S(2)}) async-start(), calls=%async_computation.1 | async-start | bytes 4194304 | tf_op jit(solution)/shard_map/while/body/eval_jaxpr/psum | solution.py:63
  650.6 6.4 collective-permute-start
  657.1 143.7 %all-reduce.3.cloned.1.call-start = ((), (), s32[]{:S(2)}) async-start(), calls=%async_computation | async-start | bytes 4194304 | tf_op jit(solution)/shard_map/while/body/eval_jaxpr/psum | solution.py:58
  726.5 139.8 %all-reduce.5.cloned.1.call-start = ((), (), s32[]{:S(2)}) async-start(), calls=%async_computation.1 | async-start | bytes 4194304 | tf_op jit(solution)/shard_map/while/body/eval_jaxpr/psum | solution.py:63
  870.3 6.4 collective-permute-start
  876.7 143.7 %all-reduce.3.cloned.1.call-start = ((), (), s32[]{:S(2)}) async-start(), calls=%async_computation | async-start | bytes 4194304 | tf_op jit(solution)/shard_map/while/body/eval_jaxpr/psum | solution.py:58
  946.1 139.8 %all-reduce.5.cloned.1.call-start = ((), (), s32[]{:S(2)}) async-start(), calls=%async_computation.1 | async-start | bytes 4194304 | tf_op jit(solution)/shard_map/while/body/eval_jaxpr/psum | solution.py:63
  1089.9 6.4 collective-permute-start
  1096.3 143.7 %all-reduce.3.cloned.1.call-start = ((), (), s32[]{:S(2)}) async-start(), calls=%async_computation | async-start | bytes 4194304 | tf_op jit(solution)/shard_map/while/body/eval_jaxpr/psum | solution.py:58
  1165.8 139.8 %all-reduce.5.cloned.1.call-start = ((), (), s32[]{:S(2)}) async-start(), calls=%async_computation.1 | async-start | bytes 4194304 | tf_op jit(solution)/shard_map/while/body/eval_jaxpr/psum | solution.py:63
  1309.5 6.4 collective-permute-start
  1316.0 143.7 %all-reduce.3.cloned.1.call-start = ((), (), s32[]{:S(2)}) async-start(), calls=%async_computation | async-start | bytes 4194304 | tf_op jit(solution)/shard_map/while/body/eval_jaxpr/psum | solution.py:58
  1385.4 139.8 %all-reduce.5.cloned.1.call-start = ((), (), s32[]{:S(2)}) async-start(), calls=%async_computation.1 | async-start | bytes 4194304 | tf_op jit(solution)/shard_map/while/body/eval_jaxpr/psum | solution.py:63
  1529.2 6.4 collective-permute-start
  1535.6 143.7 %all-reduce.3.cloned.1.call-start = ((), (), s32[]{:S(2)}) async-start(), calls=%async_computation | async-start | bytes 4194304 | tf_op jit(solution)/shard_map/while/body/eval_jaxpr/psum | solution.py:58
  1605.1 139.8 %all-reduce.5.cloned.1.call-start = ((), (), s32[]{:S(2)}) async-start(), calls=%async_computation.1 | async-start | bytes 4194304 | tf_op jit(solution)/shard_map/while/body/eval_jaxpr/psum | solution.py:63
  1748.8 6.4 collective-permute-start
  1755.3 143.7 %all-reduce.3.cloned.1.call-start = ((), (), s32[]{:S(2)}) async-start(), calls=%async_computation | async-start | bytes 4194304 | tf_op jit(solution)/shard_map/while/body/eval_jaxpr/psum | solution.py:58
  1824.7 139.8 %all-reduce.5.cloned.1.call-start = ((), (), s32[]{:S(2)}) async-start(), calls=%async_computation.1 | async-start | bytes 4194304 | tf_op jit(solution)/shard_map/while/body/eval_jaxpr/psum | solution.py:63
  1968.4 6.4 collective-permute-start
  1974.9 143.7 %all-reduce.3.cloned.1.call-start = ((), (), s32[]{:S(2)}) async-start(), calls=%async_computation | async-start | bytes 4194304 | tf_op jit(solution)/shard_map/while/body/eval_jaxpr/psum | solution.py:58
  2044.3 139.8 %all-reduce.5.cloned.1.call-start = ((), (), s32[]{:S(2)}) async-start(), calls=%async_computation.1 | async-start | bytes 4194304 | tf_op jit(solution)/shard_map/while/body/eval_jaxpr/psum | solution.py:63
  2194.5 143.7 %all-reduce.3.cloned.1.call-start = ((), (), s32[]{:S(2)}) async-start(), calls=%async_computation | async-start | bytes 4194304 | tf_op jit(solution)/shard_map/while/body/eval_jaxpr/psum | solution.py:58
  2264.0 139.8 %all-reduce.5.cloned.1.call-start = ((), (), s32[]{:S(2)}) async-start(), calls=%async_computation.1 | async-start | bytes 4194304 | tf_op jit(solution)/shard_map/while/body/eval_jaxpr/psum | solution.py:63
  2407.7 6.4 collective-permute-start
  (33 other events, 107.2 us)
Sparse Core Ops, SparseCore 0:
  86.0 55.8 all-reduce.2
  154.2 53.1 all-reduce.4
  287.4 74.0 all-reduce.2
  373.9 53.1 all-reduce.4
  507.0 74.0 all-reduce.2
  593.5 53.1 all-reduce.4
  726.6 74.0 all-reduce.2
  813.1 53.1 all-reduce.4
  946.3 74.0 all-reduce.2
  1032.8 53.1 all-reduce.4
  1165.9 74.0 all-reduce.2
  1252.4 53.1 all-reduce.4
  1385.5 74.0 all-reduce.2
  1472.0 53.1 all-reduce.4
  1605.2 74.0 all-reduce.2
  1691.7 53.1 all-reduce.4
  1824.8 74.0 all-reduce.2
  1911.3 53.1 all-reduce.4
  2044.5 74.0 all-reduce.2
  2131.0 53.1 all-reduce.4
  2264.1 74.0 all-reduce.2
  2350.6 53.1 all-reduce.4
where the time goes:
time: 2450 us; the launch traced here: 2420 us
  waiting for transfers between devices  1390 us (57%)
  matrix products  612 us (25%)
  other arithmetic  230 us (9%)
  local copies, waits for them, and re-layouts  99.8 us (4%)
  loops' own time  64.8 us (3%)
    psum x11, waiting for transfers between devices, stage_layer(): attn_sum = lax.psum(attn_part.reshape(tokens_n, model_n), 'tp')  797 us
    psum x11, waiting for transfers between devices, stage_layer(): mlp_sum = lax.psum(mlp_part, 'tp')  587 us
    dot_general x88, matrix products, one_block(): jnp.einsum('bhqk,bkhe->bqhe', prob_bf, val_all, preferred_element_type=jn...  244 us
    sub x88, matrix products, one_block(): prob_bf = jax.nn.softmax(scores, axis=-1).astype(jnp.bfloat16)  204 us
    dot_general x11, matrix products, stage_layer(): jnp.dot(hidden_act, w_down, preferred_element_type=jnp.float32)  92.7 us
    reduce_sum x22, other arithmetic, layer_norm(): mean_val = jnp.mean(val_f, axis=-1, keepdims=True)  65.3 us
    another operation x11, loops' own time, attention(): return lax.map(one_block, jnp.arange(seq_n // blk_len))  62.8 us
    dynamic_slice x88, local copies, waits for them, and re-layouts, attention(): return lax.map(one_block, jnp.arange(seq_n // blk_len))  57 us
  transfers between devices with their start and end apart: 33, of which 22 were waited for; matrix products, arithmetic and copies ran while one was open for 2% of the time, Pallas kernels for 0%

commit v1 on v0

v1 whole, which is shorter than its diff:
```python
import functools
import math

import jax
import jax.numpy as jnp
import numpy as np
from jax import lax
from jax.experimental import pallas as pl
from jax.experimental.pallas import tpu as pltpu
from jax.sharding import PartitionSpec as P

MESH = pl.DeviceIdType.MESH
UNIT = 128
KBLK = 256
LAG = 3
NEG = -1e30


def alibi_slopes(heads_n):
    closest = 2 ** int(math.floor(math.log2(heads_n)))
    base_rate = 2.0 ** (-8.0 / closest)
    slope_list = [base_rate ** (head_idx + 1) for head_idx in range(closest)]
    extra_rate = 2.0 ** (-4.0 / closest)
    slope_list = slope_list + [extra_rate ** (2 * head_idx + 1) for head_idx in range(min(closest, heads_n - closest))]
    return np.array(slope_list, dtype=np.float32)


def split_bf16(value):
    parts = []
    rest = np.float32(value)
    for _ in range(3):
        part = rest.astype(jnp.bfloat16).astype(np.float32)
        parts.append(float(part))
        rest = np.float32(rest - part)
    return parts


def layer_norm(x, gain, shift):
    mean = jnp.mean(x, axis=-1, keepdims=True)
    cent = x - mean
    var = jnp.mean(cent * cent, axis=-1, keepdims=True)
    return (cent * lax.rsqrt(var + 1e-5) * gain + shift).astype(jnp.bfloat16)


def gelu(x):
    inner = math.sqrt(2.0 / math.pi) * (x + 0.044715 * (x * x * x))
    return 0.5 * x * (1.0 + jnp.tanh(inner))


def kernel(heads_n, x_hbm, lens, wqkv_in, wout_in, wup_in, wdn_in, pack_in, out,
           wqkv, wout, wup, wdn, packs, rl_qkv, rl_out, rl_up, rl_dn,
           xbuf, ybuf, kc, vt, kx, qaug, cmask, sbuf, abuf, ctx, hbuf, ubuf,
           loc_sem, w_recv, fwd_send, rl_send, rl_recv, dir_send, pk_send,
           x0_sem, x_recv, s_send, od_send, da_send, db_send, fa_send, fb_send,
           rr_recv, rr_send, o_recv):
    tp_n = 4
    units = xbuf.shape[0]
    model = xbuf.shape[2]
    seq = units * UNIT
    quarter = wqkv.shape[3]
    hid_q = wup.shape[2]
    pairs = model // 128

    r = lax.axis_index("tp")
    p = lax.axis_index("pp")
    x = p // 2
    c = p % 2
    odd = (r + x) % 2
    layer = 2 * x + odd
    home = odd == c
    rp, rm, ro = (r + 1) % tp_n, (r + 3) % tp_n, (r + 2) % tp_n
    partner = 2 * x + (1 - c)
    sig = 1 - 2 * c
    r_fwd = (r + sig + tp_n) % tp_n
    r_bwd = (r - sig + tp_n) % tp_n
    stage0, stage1 = 2 * x, 2 * x + 1
    x_n = 4

    def micro_of(row, core, lay):
        hops = (lay + 1) // 2
        return 2 * (((row + 8 - (1 - 2 * core) * hops) % tp_n) // 2) + core

    m = micro_of(r, c, layer)

    def rcopy(src, dst, ssem, rsem, **dev):
        return pltpu.make_async_remote_copy(src_ref=src, dst_ref=dst, send_sem=ssem, recv_sem=rsem,
                                            device_id=dev, device_id_type=MESH)

    barrier = pltpu.get_barrier_semaphore()
    for dr in range(tp_n):
        for dc in range(2):
            if dr or dc:
                pl.semaphore_signal(barrier, inc=1, device_id={"tp": (r + dr) % tp_n, "pp": 2 * x + (c + dc) % 2}, device_id_type=MESH)
    for dx in (1, x_n - 1):
        pl.semaphore_signal(barrier, inc=1, device_id={"pp": 2 * ((x + dx) % x_n) + c}, device_id_type=MESH)
    pl.semaphore_wait(barrier, 9)

    def wsrc(k, h=None):
        if k == 0:
            return wqkv_in if h is None else wqkv_in.at[:, pl.ds(h * (model // 2), model // 2), :]
        ref = (None, wout_in, wup_in, wdn_in, pack_in)[k]
        if h is None:
            return ref
        half = ref.shape[0] // 2
        return ref.at[pl.ds(h * half, half)]

    def wdst(k, q, h=None):
        if k == 0:
            return wqkv.at[q] if h is None else wqkv.at[q, :, pl.ds(h * (model // 2), model // 2), :]
        if k == 2:
            return wup.at[q] if h is None else wup.at[q, pl.ds(h * (model // 2), model // 2)]
        if k == 4:
            return packs.at[q]
        ref, rows = (wout, quarter) if k == 1 else (wdn, hid_q)
        if h is None:
            return ref.at[pl.ds(pl.multiple_of(q * rows, rows), rows)]
        half = rows // 2
        return ref.at[pl.ds(pl.multiple_of(q * rows + h * half, half), half)]

    def rl(k, h):
        return (rl_qkv, rl_out, rl_up, rl_dn)[k].at[h]

    def wwait(view, sem):
        rcopy(view, view, sem, sem, pp=partner).wait_recv()

    @pl.when(home)
    def _():
        rcopy(wsrc(4), wdst(4, r), pk_send.at[0], w_recv.at[2, 4, 0], tp=ro).start()
        for k in range(4):
            rcopy(wsrc(k, 0), rl(k, 0), rl_send.at[0, k], rl_recv.at[0, k], tp=rp).start()
            rcopy(wsrc(k, 1), rl(k, 1), rl_send.at[1, k], rl_recv.at[1, k], tp=rm).start()
        for k in range(5):
            pltpu.make_async_copy(wsrc(k), wdst(k, r), loc_sem.at[k]).start()
            rcopy(wsrc(k), wdst(k, r), fwd_send.at[k], w_recv.at[0, k, 0], pp=partner).start()

    @pl.when(jnp.logical_not(home))
    def _():
        for k in (4, 0, 1, 2, 3):
            rcopy(wsrc(k), wdst(k, r), dir_send.at[0, k], w_recv.at[3, k, 0], tp=rp).start()
            rcopy(wsrc(k), wdst(k, r), dir_send.at[1, k], w_recv.at[1, k, 0], tp=rm).start()

    @pl.when(layer == 0)
    def _():
        for u in range(units):
            pltpu.make_async_copy(x_hbm.at[m, pl.ds(u * UNIT, UNIT)], xbuf.at[u], x0_sem.at[u]).start()

    kc[...] = jnp.zeros_like(kc)
    vt[...] = jnp.zeros_like(vt)
    length = lens[m]
    key = lax.broadcasted_iota(jnp.int32, (seq, 128), 0)
    lane = lax.broadcasted_iota(jnp.int32, (seq, 128), 1)
    high = (key // 256) * 256
    part = jnp.where(lane % 2 == 0, high, key - high).astype(jnp.float32)
    dead = jnp.where(key >= length, NEG, 0.0)
    kx[...] = jnp.where(lane < 6, part, jnp.where(lane == 6, dead, 0.0)).astype(jnp.bfloat16)
    slopes = alibi_slopes(heads_n)
    row = lax.broadcasted_iota(jnp.int32, (128, 256), 0)
    second = lax.broadcasted_iota(jnp.int32, (128, 256), 1) >= 128
    for pair in range(pairs):
        (h0, m0, l0), (h1, m1, l1) = split_bf16(slopes[2 * pair]), split_bf16(slopes[2 * pair + 1])
        hi, mid, low = jnp.where(second, h1, h0), jnp.where(second, m1, m0), jnp.where(second, l1, l0)
        val = jnp.where(row < 2, hi, jnp.where(row < 4, mid, jnp.where(row < 6, low, jnp.where(row == 6, 1.0, 0.0))))
        qaug[pair, 128:, :] = val.astype(jnp.bfloat16)
    kpos = lax.broadcasted_iota(jnp.int32, (KBLK, 256), 0)
    qpos = lax.broadcasted_iota(jnp.int32, (KBLK, 256), 1) % 128
    cmask[0] = jnp.where(kpos <= qpos, 0.0, NEG)
    cmask[1] = jnp.where(kpos <= qpos + 128, 0.0, NEG)

    @pl.when(home)
    def _():
        idx = 5
        for k in (4, 0, 1, 2, 3):
            for d, q in ((1, rp), (3, rm)):
                wwait(wdst(k, q), w_recv.at[d, k, 0])
                rcopy(wdst(k, q), wdst(k, q), fwd_send.at[idx], w_recv.at[d, k, 0], pp=partner).start()
                idx += 1
        wwait(wdst(4, ro), w_recv.at[2, 4, 0])
        rcopy(wdst(4, ro), wdst(4, ro), fwd_send.at[idx], w_recv.at[2, 4, 0], pp=partner).start()
        idx += 1
        for k in range(4):
            for h in range(2):
                wwait(wdst(k, ro, h), w_recv.at[2, k, h])
                rcopy(wdst(k, ro, h), wdst(k, ro, h), fwd_send.at[idx], w_recv.at[2, k, h], pp=partner).start()
                idx += 1
        for k in range(5):
            pltpu.make_async_copy(wsrc(k), wdst(k, r), loc_sem.at[k]).wait()

    @pl.when(jnp.logical_not(home))
    def _():
        for k in range(4):
            wwait(rl(k, 0), rl_recv.at[0, k])
            rcopy(rl(k, 0), wdst(k, rm, 0), rl_send.at[0, k], w_recv.at[2, k, 0], tp=rp).start()
            wwait(rl(k, 1), rl_recv.at[1, k])
            rcopy(rl(k, 1), wdst(k, rp, 1), rl_send.at[1, k], w_recv.at[2, k, 1], tp=rm).start()
        for k in range(5):
            for d, q in ((0, r), (1, rp), (3, rm)):
                wwait(wdst(k, q), w_recv.at[d, k, 0])
        wwait(wdst(4, ro), w_recv.at[2, 4, 0])
        for k in range(4):
            for h in range(2):
                wwait(wdst(k, ro, h), w_recv.at[2, k, h])

    def out_at(mm, u):
        return out.at[mm, pl.ds(pl.multiple_of(u * UNIT, UNIT), UNIT)]

    m_a = micro_of(rm, 0, stage1)
    m_b = micro_of(rp, 1, stage1)
    relay = jnp.logical_and(odd == 0, c == 1)

    def relay_unit(v):
        wwait(out_at(m_a, v), rr_recv.at[0, v])
        rcopy(out_at(m_a, v), out_at(m_a, v), rr_send.at[0, v], o_recv, tp=rp).start()
        wwait(out_at(m_b, v), rr_recv.at[1, v])
        rcopy(out_at(m_b, v), out_at(m_b, v), rr_send.at[1, v], o_recv, tp=rm).start()

    def attention(nb, diag):
        def one_pair(pair, carry):
            col = pl.ds(pl.multiple_of(pair * 128, 128), 128)
            q_rhs = qaug[pair]
            top = None
            for b in range(nb):
                keys = jnp.concatenate([kc[b * KBLK:(b + 1) * KBLK, col], kx[b * KBLK:(b + 1) * KBLK, :]], axis=1)
                s = jnp.dot(keys, q_rhs, preferred_element_type=jnp.float32)
                if b == nb - 1:
                    s = s + diag
                sbuf[b] = s
                peak = jnp.max(s, axis=0, keepdims=True)
                top = peak if top is None else jnp.maximum(top, peak)
            total = None
            acc = None
            for b in range(nb):
                e = jnp.exp(sbuf[b] - top)
                part_sum = jnp.sum(e, axis=0, keepdims=True)
                total = part_sum if total is None else total + part_sum
                pv = jnp.dot(vt[col, b * KBLK:(b + 1) * KBLK], e.astype(jnp.bfloat16), preferred_element_type=jnp.float32)
                acc = pv if acc is None else acc + pv
            acc = acc * (1.0 / total)
            both = jnp.concatenate([acc[:64, :128], acc[64:, 128:]], axis=0)
            ctx[:, col] = both.T.astype(jnp.bfloat16)
            return carry

        lax.fori_loop(0, pairs, one_pair, 0, unroll=2)

    def unit_step(u, carry):
        tok = pl.ds(pl.multiple_of(u * UNIT, UNIT), UNIT)

        @pl.when(layer == 0)
        def _():
            pltpu.make_async_copy(x_hbm.at[m, tok], xbuf.at[u], x0_sem.at[u]).wait()

        @pl.when(layer > 0)
        def _():
            wwait(xbuf.at[u], x_recv.at[u])

        @pl.when(odd == 1)
        def _():
            @pl.when(c == 0)
            def _():
                pltpu.make_async_copy(xbuf.at[u], out_at(m, u), o_recv).start()

            @pl.when(c == 1)
            def _():
                rcopy(xbuf.at[u], out_at(m, u), fa_send.at[u], o_recv, pp=stage0).start()

            rcopy(xbuf.at[u], out_at(m, u), fb_send.at[u], o_recv, tp=r_fwd, pp=stage0).start()

        xin = xbuf[u].astype(jnp.float32)
        abuf[...] = layer_norm(xin, packs[0, 0:1, :], packs[0, 1:2, :])
        head_row = lax.broadcasted_iota(jnp.int32, (128, 128), 0) < 64
        for q in range(tp_n):
            for j in range(3):
                o = jnp.dot(abuf[...], wqkv[q, j], preferred_element_type=jnp.float32)
                o = (o + packs[q, 7:8, j * quarter:(j + 1) * quarter]).astype(jnp.bfloat16)
                if j == 0:
                    o = o.astype(jnp.float32) * 0.125
                    for half in range(quarter // 128):
                        q_t = o[:, half * 128:(half + 1) * 128].T
                        pair = q * (quarter // 128) + half
                        qaug[pair, :128, :128] = jnp.where(head_row, q_t, 0.0).astype(jnp.bfloat16)
                        qaug[pair, :128, 128:] = jnp.where(head_row, 0.0, q_t).astype(jnp.bfloat16)
                elif j == 1:
                    kc[tok, q * quarter:(q + 1) * quarter] = o
                else:
                    vt[q * quarter:(q + 1) * quarter, tok] = o.astype(jnp.float32).T.astype(jnp.bfloat16)

        for nb in range(1, seq // KBLK + 1):
            @pl.when(u // 2 + 1 == nb)
            def _():
                attention(nb, cmask[u % 2])

        for n in range(model // quarter):
            cols = slice(n * quarter, (n + 1) * quarter)
            attn = jnp.dot(ctx[...], wout[:, cols], preferred_element_type=jnp.float32)
            hbuf[:, cols] = (xbuf[u, :, cols].astype(jnp.float32) + attn + packs[0, 2:3, cols]).astype(jnp.bfloat16)
        abuf[...] = layer_norm(hbuf[...].astype(jnp.float32), packs[0, 3:4, :], packs[0, 4:5, :])
        for q in range(tp_n):
            for n in range(hid_q // quarter):
                cols = slice(n * quarter, (n + 1) * quarter)
                up = jnp.dot(abuf[...], wup[q, :, cols], preferred_element_type=jnp.float32)
                up = up + packs[q, 6:7, cols]
                ubuf[:, q * hid_q + n * quarter:q * hid_q + (n + 1) * quarter] = gelu(up).astype(jnp.bfloat16)
        for n in range(model // quarter):
            cols = slice(n * quarter, (n + 1) * quarter)
            down = jnp.dot(ubuf[...], wdn[:, cols], preferred_element_type=jnp.float32)
            ybuf[u, :, cols] = (hbuf[:, cols].astype(jnp.float32) + down + packs[0, 5:6, cols]).astype(jnp.bfloat16)

        @pl.when(odd == 0)
        def _():
            rcopy(ybuf.at[u], xbuf.at[u], s_send.at[u], x_recv.at[u], tp=r_fwd).start()
            rcopy(ybuf.at[u], out_at(m, u), da_send.at[u], o_recv, tp=r_bwd, pp=stage0).start()

            @pl.when(c == 0)
            def _():
                pltpu.make_async_copy(ybuf.at[u], out_at(m, u), o_recv).start()

            @pl.when(c == 1)
            def _():
                rcopy(ybuf.at[u], out_at(m, u), od_send.at[u], o_recv, pp=stage0).start()

        @pl.when(odd == 1)
        def _():
            @pl.when(x < x_n - 1)
            def _():
                rcopy(ybuf.at[u], xbuf.at[u], s_send.at[u], x_recv.at[u], pp=(p + 2) % (2 * x_n)).start()

            rcopy(ybuf.at[u], out_at(m, u), da_send.at[u], rr_recv.at[c, u], tp=r_fwd, pp=stage1).start()
            rcopy(ybuf.at[u], out_at(m, u), db_send.at[u], o_recv, tp=r_bwd, pp=stage1).start()

            @pl.when(c == 1)
            def _():
                pltpu.make_async_copy(ybuf.at[u], out_at(m, u), o_recv).start()

            @pl.when(c == 0)
            def _():
                rcopy(ybuf.at[u], out_at(m, u), od_send.at[u], o_recv, pp=stage1).start()

        @pl.when(jnp.logical_and(relay, u >= LAG))
        def _():
            relay_unit(u - LAG)

        return carry

    lax.fori_loop(0, units, unit_step, 0)

    @pl.when(relay)
    def _():
        for v in range(max(0, units - LAG), units):
            relay_unit(v)

    def sent(view, sem):
        rcopy(view, view, sem, sem, pp=partner).wait_send()

    @pl.when(home)
    def _():
        sent(wsrc(4), pk_send.at[0])
        for k in range(4):
            sent(rl(k, 0), rl_send.at[0, k])
            sent(rl(k, 1), rl_send.at[1, k])
        for k in range(5):
            sent(wsrc(k), fwd_send.at[k])
        idx = 5
        for k in (4, 0, 1, 2, 3):
            for d in range(2):
                sent(wsrc(k), fwd_send.at[idx])
                idx += 1
        sent(wsrc(4), fwd_send.at[idx])
        idx += 1
        for k in range(4):
            for h in range(2):
                sent(wsrc(k, h), fwd_send.at[idx])
                idx += 1

    @pl.when(jnp.logical_not(home))
    def _():
        for k in range(5):
            for d in range(2):
                sent(wsrc(k), dir_send.at[d, k])
        for k in range(4):
            for d in range(2):
                sent(rl(k, d), rl_send.at[d, k])

    def drain(u, carry):
        @pl.when(odd == 0)
        def _():
            sent(ybuf.at[u], s_send.at[u])
            sent(ybuf.at[u], da_send.at[u])

            @pl.when(c == 1)
            def _():
                sent(ybuf.at[u], od_send.at[u])
                sent(ybuf.at[u], rr_send.at[0, u])
                sent(ybuf.at[u], rr_send.at[1, u])

        @pl.when(odd == 1)
        def _():
            @pl.when(x < x_n - 1)
            def _():
                sent(ybuf.at[u], s_send.at[u])

            sent(ybuf.at[u], da_send.at[u])
            sent(ybuf.at[u], db_send.at[u])
            sent(ybuf.at[u], fb_send.at[u])

            @pl.when(c == 0)
            def _():
                sent(ybuf.at[u], od_send.at[u])

            @pl.when(c == 1)
            def _():
                sent(ybuf.at[u], fa_send.at[u])

        return carry

    lax.fori_loop(0, units, drain, 0)

    @pl.when(relay)
    def _():
        wwait(out.at[pl.ds(0, out.shape[0] // 2)], o_recv)

    @pl.when(jnp.logical_not(relay))
    def _():
        wwait(out, o_recv)


def solution(mesh):
    tp_size = mesh.shape['tp']
    in_specs = (P('dp'), P('dp'), P('pp'), P('pp'), P('pp', None, None, 'tp'), P('pp', None, 'tp', None), P('pp', 'tp', None), P('pp'), P('pp'), P('pp'), P('pp', None, 'tp'), P('pp', 'tp'), P('pp', 'tp', None), P('pp'))

    def per_device(x_in, seq_lens, ln1_gain, ln1_shift, w_qkv, b_qkv, w_out, b_out, ln2_gain, ln2_shift, w_up, b_up, w_down, b_down):
        micro_n, batch_n, seq_n, model_n = x_in.shape
        heads_n = b_qkv.shape[2] * tp_size
        quarter = w_qkv.shape[3]
        hid_q = w_up.shape[2]
        bf16, f32 = jnp.bfloat16, jnp.float32
        wqkv_t = jnp.transpose(w_qkv[0], (1, 0, 2))
        b_qkv_row = jnp.pad(b_qkv.reshape(1, 3 * quarter), ((0, 0), (0, model_n - 3 * quarter)))
        pack = jnp.concatenate([ln1_gain, ln1_shift, b_out, ln2_gain, ln2_shift, b_down, b_up, b_qkv_row], axis=0).astype(f32)
        units = seq_n // UNIT
        pairs = model_n // 128
        dma = pltpu.SemaphoreType.DMA
        anywhere = pl.BlockSpec(memory_space=pl.ANY)
        tokens = batch_n * seq_n
        out = pl.pallas_call(
            functools.partial(kernel, heads_n),
            out_shape=jax.ShapeDtypeStruct((micro_n, tokens, model_n), bf16),
            in_specs=[anywhere, pl.BlockSpec(memory_space=pltpu.SMEM)] + [anywhere] * 5,
            out_specs=anywhere,
            scratch_shapes=[
                pltpu.VMEM((tp_size, 3, model_n, quarter), bf16),
                pltpu.VMEM((tp_size * quarter, model_n), bf16),
                pltpu.VMEM((tp_size, model_n, hid_q), bf16),
                pltpu.VMEM((tp_size * hid_q, model_n), bf16),
                pltpu.VMEM((tp_size,) + pack.shape, f32),
                pltpu.VMEM((2, 3, model_n // 2, quarter), bf16),
                pltpu.VMEM((2, quarter // 2, model_n), bf16),
                pltpu.VMEM((2, model_n // 2, hid_q), bf16),
                pltpu.VMEM((2, hid_q // 2, model_n), bf16),
                pltpu.VMEM((units, UNIT, model_n), bf16),
                pltpu.VMEM((units, UNIT, model_n), bf16),
                pltpu.VMEM((seq_n, model_n), bf16),
                pltpu.VMEM((model_n, seq_n), bf16),
                pltpu.VMEM((seq_n, 128), bf16),
                pltpu.VMEM((pairs, 256, 256), bf16),
                pltpu.VMEM((2, KBLK, 256), f32),
                pltpu.VMEM((seq_n // KBLK, KBLK, 256), f32),
                pltpu.VMEM((UNIT, model_n), bf16),
                pltpu.VMEM((UNIT, model_n), bf16),
                pltpu.VMEM((UNIT, model_n), bf16),
                pltpu.VMEM((UNIT, tp_size * hid_q), bf16),
                dma((5,)), dma((4, 5, 2)), dma((24,)), dma((2, 4)), dma((2, 4)), dma((2, 5)), dma((1,)),
                dma((units,)), dma((units,)), dma((units,)), dma((units,)), dma((units,)), dma((units,)), dma((units,)), dma((units,)),
                dma((2, units)), dma((2, units)), dma,
            ],
            compiler_params=pltpu.CompilerParams(collective_id=0, has_side_effects=True, vmem_limit_bytes=63 * 1024 * 1024),
            cost_estimate=pl.CostEstimate(flops=30 * 10 ** 9, bytes_accessed=40 * 10 ** 6, transcendentals=10 ** 7),
        )(x_in.reshape(micro_n, tokens, model_n), seq_lens.reshape(micro_n * batch_n), wqkv_t, w_out[0], w_up[0], w_down[0], pack)
        return out.reshape((1,) + x_in.shape)

    return jax.shard_map(per_device, mesh=mesh, in_specs=in_specs, out_specs=P('pp', 'dp'), check_vma=False)
```

time: 2450 us -> 346 us (0.14); the launches traced: 2420 us -> 346 us
  waiting for transfers between devices: 1390 us -> 0 us
  matrix products: 612 us -> 0 us
  Pallas kernels: 0 us -> 336 us
  other arithmetic: 230 us -> 0.62 us
  local copies, waits for them, and re-layouts: 99.8 us -> 9.38 us
  loops' own time: 64.8 us -> 0 us
    psum x22 -> x0, waiting for transfers between devices: 1380 us -> none  [the longest x11 797 us: stage_layer(): attn_sum = lax.psum(attn_part.reshape(tokens_n, model_n), 'tp')]
    dot_general x121 -> x0, matrix products: 408 us -> none  [the longest x88 244 us: one_block(): jnp.einsum('bhqk,bkhe->bqhe', prob_bf, val_all, preferred_element_type=jn...]
    pallas_call x0 -> x1, Pallas kernels: none -> 336 us  [per_device(): pl.pallas_call(functools.partial(kernel, heads_n), out_shape=jax.ShapeDty...]
    sub x88 -> x0, matrix products: 204 us -> none  [one_block(): prob_bf = jax.nn.softmax(scores, axis=-1).astype(jnp.bfloat16)]
    dynamic_slice x111 -> x0, local copies, waits for them, and re-layouts: 85.3 us -> none  [the longest x88 57 us: attention(): return lax.map(one_block, jnp.arange(seq_n // blk_len))]
    reduce_sum x44 -> x0, other arithmetic: 80.5 us -> none  [the longest x22 65.3 us: layer_norm(): mean_val = jnp.mean(val_f, axis=-1, keepdims=True)]
    another operation x12 -> x0, loops' own time: 64.8 us -> none  [the longest x11 62.8 us: attention(): return lax.map(one_block, jnp.arange(seq_n // blk_len))]
    lt x88 -> x0, other arithmetic: 51.3 us -> none  [attention(): key_ok = key_pos[None, :] < lens_row[:, None]]
  transfers between devices with their start and end apart: 33 -> 0, of which waited for: 22 -> 0; matrix products, arithmetic and copies ran while one was open for 2% -> 0% of each run, Pallas kernels for 0% -> 0%
where the time goes in v1:
time: 346 us
  Pallas kernels  336 us (97%)
  local copies, waits for them, and re-layouts  9.38 us (3%)
    pallas_call x1, Pallas kernels, per_device(): pl.pallas_call(functools.partial(kernel, heads_n), out_shape=jax.ShapeDty...  336 us
    unnamed x1, local copies, waits for them, and re-layouts  7.76 us

profile of v1, /device:TPU:103, one launch (start us, length us, event | category | flops | bytes accessed | tf_op | source)
XLA Modules:
  0.0 346.1 jit_solution(10720703650430584309)
XLA Ops:
  0.0 0.8 reshape.14
  0.8 0.8 concatenate.3
  1.6 0.6 convert_element_type.5.pack_in
  2.2 336.1 %shard_map.136 = bf16[4,1024,1024]{2,1,0:T(8,128)(2,1)} custom-call(bf16[4,1024,1024]{2,1,0:T(8,128)(2,1)} %bitcast.12, s32[4]{0:T(128)} %bitcast.17, bf16[3,1024,256]{2,1,0:T(8,128)(2,1)} %bitcast.15, bf16[256,1024]{1,0:T(8,128)(2,1)} %bitcast.16, bf16[1024,1024]{1,0:T(8,128)(2,1)} %bitcast.13, bf16[1024,1024]{1,0:T(8,128)(2,1)} %bitcast.14, ...), custom_call_target="tpu_custom_call" | custom-call | flops 30000001024 | bytes 40000000 | tf_op jit(solution)/shard_map/pallas_call | solution.py:443
  338.4 7.8 %copy.17 = bf16[1,4,1,1024,1024]{4,3,2,1,0:T(8,128)(2,1)} copy(bf16[1,4,1,1024,1024]{4,3,2,1,0:T(8,128)(2,1)} %bitcast.11) | data formatting | bytes 16777216
  (1 shorter events, 0.0 us)

commit v2 on v1

--- a/solution.py
+++ b/solution.py
@@ -12,7 +12,7 @@
 MESH = pl.DeviceIdType.MESH
 UNIT = 128
 KBLK = 256
-LAG = 3
+LAG = 4
 NEG = -1e30
 
 
@@ -214,22 +214,25 @@
         rcopy(out_at(m_b, v), out_at(m_b, v), rr_send.at[1, v], o_recv, tp=rm).start()
 
     def attention(nb, diag):
-        def one_pair(pair, carry):
-            col = pl.ds(pl.multiple_of(pair * 128, 128), 128)
-            q_rhs = qaug[pair]
+        def scores(pair):
+            col = slice(pair * 128, (pair + 1) * 128)
             top = None
             for b in range(nb):
                 keys = jnp.concatenate([kc[b * KBLK:(b + 1) * KBLK, col], kx[b * KBLK:(b + 1) * KBLK, :]], axis=1)
-                s = jnp.dot(keys, q_rhs, preferred_element_type=jnp.float32)
+                s = jnp.dot(keys, qaug[pair], preferred_element_type=jnp.float32)
                 if b == nb - 1:
                     s = s + diag
-                sbuf[b] = s
+                sbuf[pair % 2, b] = s
                 peak = jnp.max(s, axis=0, keepdims=True)
                 top = peak if top is None else jnp.maximum(top, peak)
+            return top
+
+        def weigh(pair, top):
+            col = slice(pair * 128, (pair + 1) * 128)
             total = None
             acc = None
             for b in range(nb):
-                e = jnp.exp(sbuf[b] - top)
+                e = jnp.exp(sbuf[pair % 2, b] - top)
                 part_sum = jnp.sum(e, axis=0, keepdims=True)
                 total = part_sum if total is None else total + part_sum
                 pv = jnp.dot(vt[col, b * KBLK:(b + 1) * KBLK], e.astype(jnp.bfloat16), preferred_element_type=jnp.float32)
@@ -237,9 +240,30 @@
             acc = acc * (1.0 / total)
             both = jnp.concatenate([acc[:64, :128], acc[64:, 128:]], axis=0)
             ctx[:, col] = both.T.astype(jnp.bfloat16)
-            return carry
-
-        lax.fori_loop(0, pairs, one_pair, 0, unroll=2)
+
+        top = scores(0)
+        for pair in range(pairs):
+            later = scores(pair + 1) if pair + 1 < pairs else None
+            weigh(pair, top)
+            top = later
+
+    r_next = (r + (1 - odd) * sig + tp_n) % tp_n
+    p_next = (p + 2 * odd) % (2 * x_n)
+
+    def store_unit(v):
+        @pl.when(home)
+        def _():
+            pltpu.make_async_copy(ybuf.at[v], out_at(m, v), o_recv).start()
+
+        @pl.when(jnp.logical_not(home))
+        def _():
+            rcopy(ybuf.at[v], out_at(m, v), od_send.at[v], o_recv, pp=partner).start()
+
+        rcopy(ybuf.at[v], out_at(m, v), da_send.at[v], o_recv, tp=r_bwd, pp=2 * x + odd).start()
+
+        @pl.when(odd == 1)
+        def _():
+            rcopy(ybuf.at[v], out_at(m, v), db_send.at[v], rr_recv.at[c, v], tp=r_fwd, pp=stage1).start()
 
     def unit_step(u, carry):
         tok = pl.ds(pl.multiple_of(u * UNIT, UNIT), UNIT)
@@ -260,9 +284,13 @@
 
             @pl.when(c == 1)
             def _():
-                rcopy(xbuf.at[u], out_at(m, u), fa_send.at[u], o_recv, pp=stage0).start()
+                rcopy(xbuf.at[u], out_at(m, u), fa_send.at[u], o_recv, pp=partner).start()
 
             rcopy(xbuf.at[u], out_at(m, u), fb_send.at[u], o_recv, tp=r_fwd, pp=stage0).start()
+
+        @pl.when(u > 0)
+        def _():
+            store_unit(u - 1)
 
         xin = xbuf[u].astype(jnp.float32)
         abuf[...] = layer_norm(xin, packs[0, 0:1, :], packs[0, 1:2, :])
@@ -299,40 +327,12 @@
                 up = jnp.dot(abuf[...], wup[q, :, cols], preferred_element_type=jnp.float32)
                 up = up + packs[q, 6:7, cols]
                 ubuf[:, q * hid_q + n * quarter:q * hid_q + (n + 1) * quarter] = gelu(up).astype(jnp.bfloat16)
-        for n in range(model // quarter):
-            cols = slice(n * quarter, (n + 1) * quarter)
+        half_model = model // 2
+        for n in range(2):
+            cols = slice(n * half_model, (n + 1) * half_model)
             down = jnp.dot(ubuf[...], wdn[:, cols], preferred_element_type=jnp.float32)
             ybuf[u, :, cols] = (hbuf[:, cols].astype(jnp.float32) + down + packs[0, 5:6, cols]).astype(jnp.bfloat16)
-
-        @pl.when(odd == 0)
-        def _():
-            rcopy(ybuf.at[u], xbuf.at[u], s_send.at[u], x_recv.at[u], tp=r_fwd).start()
-            rcopy(ybuf.at[u], out_at(m, u), da_send.at[u], o_recv, tp=r_bwd, pp=stage0).start()
-
-            @pl.when(c == 0)
-            def _():
-                pltpu.make_async_copy(ybuf.at[u], out_at(m, u), o_recv).start()
-
-            @pl.when(c == 1)
-            def _():
-                rcopy(ybuf.at[u], out_at(m, u), od_send.at[u], o_recv, pp=stage0).start()
-
-        @pl.when(odd == 1)
-        def _():
-            @pl.when(x < x_n - 1)
-            def _():
-                rcopy(ybuf.at[u], xbuf.at[u], s_send.at[u], x_recv.at[u], pp=(p + 2) % (2 * x_n)).start()
-
-            rcopy(ybuf.at[u], out_at(m, u), da_send.at[u], rr_recv.at[c, u], tp=r_fwd, pp=stage1).start()
-            rcopy(ybuf.at[u], out_at(m, u), db_send.at[u], o_recv, tp=r_bwd, pp=stage1).start()
-
-            @pl.when(c == 1)
-            def _():
-                pltpu.make_async_copy(ybuf.at[u], out_at(m, u), o_recv).start()
-
-            @pl.when(c == 0)
-            def _():
-                rcopy(ybuf.at[u], out_at(m, u), od_send.at[u], o_recv, pp=stage1).start()
+            rcopy(ybuf.at[u, :, cols], xbuf.at[u, :, cols], s_send.at[u], x_recv.at[u], tp=r_next, pp=p_next).start()
 
         @pl.when(jnp.logical_and(relay, u >= LAG))
         def _():
@@ -341,6 +341,7 @@
         return carry
 
     lax.fori_loop(0, units, unit_step, 0)
+    store_unit(units - 1)
 
     @pl.when(relay)
     def _():
@@ -380,34 +381,30 @@
                 sent(rl(k, d), rl_send.at[d, k])
 
     def drain(u, carry):
-        @pl.when(odd == 0)
-        def _():
-            sent(ybuf.at[u], s_send.at[u])
-            sent(ybuf.at[u], da_send.at[u])
-
-            @pl.when(c == 1)
-            def _():
-                sent(ybuf.at[u], od_send.at[u])
-                sent(ybuf.at[u], rr_send.at[0, u])
-                sent(ybuf.at[u], rr_send.at[1, u])
+        sent(ybuf.at[u], s_send.at[u])
+        sent(ybuf.at[u], da_send.at[u])
+
+        @pl.when(jnp.logical_not(home))
+        def _():
+            sent(ybuf.at[u], od_send.at[u])
+
+        @pl.when(relay)
+        def _():
+            sent(ybuf.at[u], rr_send.at[0, u])
+            sent(ybuf.at[u], rr_send.at[1, u])
 
         @pl.when(odd == 1)
         def _():
-            @pl.when(x < x_n - 1)
-            def _():
-                sent(ybuf.at[u], s_send.at[u])
-
-            sent(ybuf.at[u], da_send.at[u])
             sent(ybuf.at[u], db_send.at[u])
             sent(ybuf.at[u], fb_send.at[u])
-
-            @pl.when(c == 0)
-            def _():
-                sent(ybuf.at[u], od_send.at[u])
 
             @pl.when(c == 1)
             def _():
                 sent(ybuf.at[u], fa_send.at[u])
+
+        @pl.when(layer == 0)
+        def _():
+            wwait(xbuf.at[u], x_recv.at[u])
 
         return carry
 
@@ -462,7 +459,7 @@
                 pltpu.VMEM((seq_n, 128), bf16),
                 pltpu.VMEM((pairs, 256, 256), bf16),
                 pltpu.VMEM((2, KBLK, 256), f32),
-                pltpu.VMEM((seq_n // KBLK, KBLK, 256), f32),
+                pltpu.VMEM((2, seq_n // KBLK, KBLK, 256), f32),
                 pltpu.VMEM((UNIT, model_n), bf16),
                 pltpu.VMEM((UNIT, model_n), bf16),
                 pltpu.VMEM((UNIT, model_n), bf16),

time: 346 us -> 322 us (0.931)
  Pallas kernels: 336 us -> 312 us
    pallas_call x1, Pallas kernels: 336 us -> 312 us  [per_device(): pl.pallas_call(functools.partial(kernel, heads_n), out_shape=jax.ShapeDty...]
where the time goes in v2:
time: 322 us
  Pallas kernels  312 us (97%)
  local copies, waits for them, and re-layouts  9.38 us (3%)
    pallas_call x1, Pallas kernels, per_device(): pl.pallas_call(functools.partial(kernel, heads_n), out_shape=jax.ShapeDty...  312 us
    unnamed x1, local copies, waits for them, and re-layouts  7.76 us

profile of v2, /device:TPU:103, one launch (start us, length us, event | category | flops | bytes accessed | tf_op | source)
XLA Modules:
  0.0 322.2 jit_solution(13585791286428820180)
XLA Ops:
  0.0 0.8 reshape.14
  0.8 0.8 concatenate.3
  1.6 0.6 convert_element_type.5.pack_in
  2.2 312.2 %shard_map.136 = bf16[4,1024,1024]{2,1,0:T(8,128)(2,1)} custom-call(bf16[4,1024,1024]{2,1,0:T(8,128)(2,1)} %bitcast.12, s32[4]{0:T(128)} %bitcast.17, bf16[3,1024,256]{2,1,0:T(8,128)(2,1)} %bitcast.15, bf16[256,1024]{1,0:T(8,128)(2,1)} %bitcast.16, bf16[1024,1024]{1,0:T(8,128)(2,1)} %bitcast.13, bf16[1024,1024]{1,0:T(8,128)(2,1)} %bitcast.14, ...), custom_call_target="tpu_custom_call" | custom-call | flops 30000001024 | bytes 40000000 | tf_op jit(solution)/shard_map/pallas_call | solution.py:440
  314.4 7.8 %copy.17 = bf16[1,4,1,1024,1024]{4,3,2,1,0:T(8,128)(2,1)} copy(bf16[1,4,1,1024,1024]{4,3,2,1,0:T(8,128)(2,1)} %bitcast.11) | data formatting | bytes 16777216
  (1 shorter events, 0.0 us)

commit v3 on v2

--- a/solution.py
+++ b/solution.py
@@ -12,7 +12,6 @@
 MESH = pl.DeviceIdType.MESH
 UNIT = 128
 KBLK = 256
-LAG = 4
 NEG = -1e30
 
 
@@ -48,10 +47,10 @@
 
 
 def kernel(heads_n, x_hbm, lens, wqkv_in, wout_in, wup_in, wdn_in, pack_in, out,
-           wqkv, wout, wup, wdn, packs, rl_qkv, rl_out, rl_up, rl_dn,
-           xbuf, ybuf, kc, vt, kx, qaug, cmask, sbuf, abuf, ctx, hbuf, ubuf,
-           loc_sem, w_recv, fwd_send, rl_send, rl_recv, dir_send, pk_send,
-           x0_sem, x_recv, s_send, od_send, da_send, db_send, fa_send, fb_send,
+           wqkv, wout, wup, wdn, packs, rl_qkv, rl_out, rl_up, rl_dn, sw_qkv, sw_out, sw_up, sw_dn, sw_pack,
+           xbuf, ybuf, kc0, kc1, kc2, kc3, vt0, vt1, vt2, vt3, kx, qaug, cmask, sbuf, abuf, ctx, hbuf, ubuf,
+           sw_send, sw_recv, w_recv, fwd_send, rl_send, rl_recv, dir_send, pk_send, go,
+           x0_sem, x_recv, s_send, od_send, da_send, db_send, fa_send, fb_send, fc_send,
            rr_recv, rr_send, o_recv):
     tp_n = 4
     units = xbuf.shape[0]
@@ -65,9 +64,12 @@
     p = lax.axis_index("pp")
     x = p // 2
     c = p % 2
-    odd = (r + x) % 2
-    layer = 2 * x + odd
+    odd = (r + (x + 1) // 2 + 1) % 2
+    even_col = x + (1 - x % 2) * (2 - 2 * x)
+    layer = odd * (2 * x + 1) + (1 - odd) * 2 * even_col
     home = odd == c
+    moved = jnp.logical_and(c == 0, x % 2 == 0)
+    early_row = r % 2 == 0
     rp, rm, ro = (r + 1) % tp_n, (r + 3) % tp_n, (r + 2) % tp_n
     partner = 2 * x + (1 - c)
     sig = 1 - 2 * c
@@ -77,7 +79,7 @@
     x_n = 4
 
     def micro_of(row, core, lay):
-        hops = (lay + 1) // 2
+        hops = (lay + 1) // 4
         return 2 * (((row + 8 - (1 - 2 * core) * hops) % tp_n) // 2) + core
 
     m = micro_of(r, c, layer)
@@ -91,14 +93,16 @@
         for dc in range(2):
             if dr or dc:
                 pl.semaphore_signal(barrier, inc=1, device_id={"tp": (r + dr) % tp_n, "pp": 2 * x + (c + dc) % 2}, device_id_type=MESH)
-    for dx in (1, x_n - 1):
+    for dx in range(1, x_n):
         pl.semaphore_signal(barrier, inc=1, device_id={"pp": 2 * ((x + dx) % x_n) + c}, device_id_type=MESH)
-    pl.semaphore_wait(barrier, 9)
+    pl.semaphore_wait(barrier, 10)
 
     def wsrc(k, h=None):
+        if k == 4:
+            return pack_in
         if k == 0:
             return wqkv_in if h is None else wqkv_in.at[:, pl.ds(h * (model // 2), model // 2), :]
-        ref = (None, wout_in, wup_in, wdn_in, pack_in)[k]
+        ref = (None, wout_in, wup_in, wdn_in)[k]
         if h is None:
             return ref
         half = ref.shape[0] // 2
@@ -120,32 +124,49 @@
     def rl(k, h):
         return (rl_qkv, rl_out, rl_up, rl_dn)[k].at[h]
 
+    def sw(k, h):
+        if k == 4:
+            return sw_pack
+        if k == 0:
+            return sw_qkv.at[:, pl.ds(h * (model // 2), model // 2), :]
+        ref = (None, sw_out, sw_up, sw_dn)[k]
+        half = ref.shape[0] // 2
+        return ref.at[pl.ds(h * half, half)]
+
     def wwait(view, sem):
         rcopy(view, view, sem, sem, pp=partner).wait_recv()
 
-    @pl.when(home)
-    def _():
-        rcopy(wsrc(4), wdst(4, r), pk_send.at[0], w_recv.at[2, 4, 0], tp=ro).start()
-        for k in range(4):
-            rcopy(wsrc(k, 0), rl(k, 0), rl_send.at[0, k], rl_recv.at[0, k], tp=rp).start()
-            rcopy(wsrc(k, 1), rl(k, 1), rl_send.at[1, k], rl_recv.at[1, k], tp=rm).start()
-        for k in range(5):
-            pltpu.make_async_copy(wsrc(k), wdst(k, r), loc_sem.at[k]).start()
-            rcopy(wsrc(k), wdst(k, r), fwd_send.at[k], w_recv.at[0, k, 0], pp=partner).start()
-
-    @pl.when(jnp.logical_not(home))
-    def _():
-        for k in (4, 0, 1, 2, 3):
-            rcopy(wsrc(k), wdst(k, r), dir_send.at[0, k], w_recv.at[3, k, 0], tp=rp).start()
-            rcopy(wsrc(k), wdst(k, r), dir_send.at[1, k], w_recv.at[1, k, 0], tp=rm).start()
+    pieces = [(4, 0), (1, 0), (1, 1), (0, 0), (0, 1), (2, 0), (2, 1), (3, 0), (3, 1)]
+    mats = pieces[1:]
+
+    @pl.when(jnp.logical_and(moved, odd == 1))
+    def _():
+        for k, h in pieces:
+            rcopy(wsrc(k, h), wdst(k, r, h), sw_send.at[k, h], sw_recv.at[k, h], pp=2 * (2 - x)).start()
+
+    @pl.when(jnp.logical_and(moved, odd == 0))
+    def _():
+        for k, h in pieces:
+            rcopy(wsrc(k, h), sw(k, h), sw_send.at[k, h], sw_recv.at[k, h], pp=2 * (2 - x)).start()
+
+    @pl.when(jnp.logical_and(jnp.logical_not(moved), home))
+    def _():
+        for k, h in pieces:
+            pltpu.make_async_copy(wsrc(k, h), wdst(k, r, h), sw_recv.at[k, h]).start()
+
+    @pl.when(jnp.logical_not(jnp.logical_or(moved, home)))
+    def _():
+        for k, h in pieces:
+            pltpu.make_async_copy(wsrc(k, h), sw(k, h), sw_recv.at[k, h]).start()
 
     @pl.when(layer == 0)
     def _():
         for u in range(units):
             pltpu.make_async_copy(x_hbm.at[m, pl.ds(u * UNIT, UNIT)], xbuf.at[u], x0_sem.at[u]).start()
 
-    kc[...] = jnp.zeros_like(kc)
-    vt[...] = jnp.zeros_like(vt)
+    kc, vt = (kc0, kc1, kc2, kc3), (vt0, vt1, vt2, vt3)
+    for ref in kc + vt:
+        ref[...] = jnp.zeros_like(ref)
     length = lens[m]
     key = lax.broadcasted_iota(jnp.int32, (seq, 128), 0)
     lane = lax.broadcasted_iota(jnp.int32, (seq, 128), 1)
@@ -166,46 +187,86 @@
     cmask[0] = jnp.where(kpos <= qpos, 0.0, NEG)
     cmask[1] = jnp.where(kpos <= qpos + 128, 0.0, NEG)
 
+    def to_relay(k, h):
+        rcopy(wdst(k, r, h), rl(k, h), rl_send.at[h, k], rl_recv.at[h, k], tp=(rp, rm)[h]).start()
+
+    def to_partner(k, q, d, h):
+        rcopy(wdst(k, q, h), wdst(k, q, h), fwd_send.at[d, k, h], w_recv.at[d, k, h], pp=partner).start()
+
+    def hand_out():
+        for k, h in pieces:
+            wwait(sw(k, h), sw_recv.at[k, h])
+            rcopy(sw(k, h), wdst(k, r, h), dir_send.at[0, k, h], w_recv.at[3, k, h], tp=rp).start()
+            rcopy(sw(k, h), wdst(k, r, h), dir_send.at[1, k, h], w_recv.at[1, k, h], tp=rm).start()
+
+    def relay_weights(k, h):
+        wwait(rl(k, h), rl_recv.at[h, k])
+        rcopy(rl(k, h), wdst(k, (rm, rp)[h], h), rl_send.at[h, k], w_recv.at[2, k, h], tp=(rp, rm)[h]).start()
+
+    def from_partner():
+        for d, q in ((0, r), (1, rp), (3, rm), (2, ro)):
+            for k, h in pieces:
+                wwait(wdst(k, q, h), w_recv.at[d, k, h])
+
+    def sent(view, sem):
+        rcopy(view, view, sem, sem, pp=partner).wait_send()
+
+    def handed_out():
+        for k, h in pieces:
+            for d in range(2):
+                sent(sw(k, h), dir_send.at[d, k, h])
+        for k, h in mats:
+            sent(rl(k, h), rl_send.at[h, k])
+
     @pl.when(home)
     def _():
-        idx = 5
-        for k in (4, 0, 1, 2, 3):
+        for k, h in pieces:
+            wwait(wdst(k, r, h), sw_recv.at[k, h])
+            if k == 4:
+                rcopy(wdst(k, r), wdst(k, r), pk_send.at[0], w_recv.at[2, k, h], tp=ro).start()
+            else:
+                @pl.when(early_row)
+                def _():
+                    to_relay(k, h)
+            to_partner(k, r, 0, h)
+
+        @pl.when(jnp.logical_not(early_row))
+        def _():
+            pl.semaphore_wait(go, 1)
+            for k, h in mats:
+                to_relay(k, h)
+
+        for k, h in pieces:
             for d, q in ((1, rp), (3, rm)):
-                wwait(wdst(k, q), w_recv.at[d, k, 0])
-                rcopy(wdst(k, q), wdst(k, q), fwd_send.at[idx], w_recv.at[d, k, 0], pp=partner).start()
-                idx += 1
-        wwait(wdst(4, ro), w_recv.at[2, 4, 0])
-        rcopy(wdst(4, ro), wdst(4, ro), fwd_send.at[idx], w_recv.at[2, 4, 0], pp=partner).start()
-        idx += 1
-        for k in range(4):
-            for h in range(2):
-                wwait(wdst(k, ro, h), w_recv.at[2, k, h])
-                rcopy(wdst(k, ro, h), wdst(k, ro, h), fwd_send.at[idx], w_recv.at[2, k, h], pp=partner).start()
-                idx += 1
-        for k in range(5):
-            pltpu.make_async_copy(wsrc(k), wdst(k, r), loc_sem.at[k]).wait()
-
-    @pl.when(jnp.logical_not(home))
-    def _():
-        for k in range(4):
-            wwait(rl(k, 0), rl_recv.at[0, k])
-            rcopy(rl(k, 0), wdst(k, rm, 0), rl_send.at[0, k], w_recv.at[2, k, 0], tp=rp).start()
-            wwait(rl(k, 1), rl_recv.at[1, k])
-            rcopy(rl(k, 1), wdst(k, rp, 1), rl_send.at[1, k], w_recv.at[2, k, 1], tp=rm).start()
-        for k in range(5):
-            for d, q in ((0, r), (1, rp), (3, rm)):
-                wwait(wdst(k, q), w_recv.at[d, k, 0])
-        wwait(wdst(4, ro), w_recv.at[2, 4, 0])
-        for k in range(4):
-            for h in range(2):
-                wwait(wdst(k, ro, h), w_recv.at[2, k, h])
+                wwait(wdst(k, q, h), w_recv.at[d, k, h])
+                to_partner(k, q, d, h)
+        for k, h in pieces:
+            wwait(wdst(k, ro, h), w_recv.at[2, k, h])
+            to_partner(k, ro, 2, h)
+
+    late_source = jnp.logical_and(early_row, jnp.logical_not(home))
+
+    @pl.when(jnp.logical_not(jnp.logical_or(home, early_row)))
+    def _():
+        hand_out()
+        for k, h in mats:
+            relay_weights(k, h)
+        handed_out()
+        pl.semaphore_signal(go, inc=1, device_id={"pp": partner}, device_id_type=MESH)
+        from_partner()
+
+    @pl.when(late_source)
+    def _():
+        from_partner()
+        hand_out()
 
     def out_at(mm, u):
         return out.at[mm, pl.ds(pl.multiple_of(u * UNIT, UNIT), UNIT)]
 
     m_a = micro_of(rm, 0, stage1)
     m_b = micro_of(rp, 1, stage1)
-    relay = jnp.logical_and(odd == 0, c == 1)
+    relay = jnp.logical_and(odd == 0, jnp.logical_or(c == 1, x % 2 == 0))
+    lag = min(5, units) * (x % 2) + units * ((x // 2) * (1 - x % 2))
 
     def relay_unit(v):
         wwait(out_at(m_a, v), rr_recv.at[0, v])
@@ -213,12 +274,31 @@
         wwait(out_at(m_b, v), rr_recv.at[1, v])
         rcopy(out_at(m_b, v), out_at(m_b, v), rr_send.at[1, v], o_recv, tp=rm).start()
 
-    def attention(nb, diag):
+    def attention(nb, diag, tok):
+        per_q = quarter // 128
+        head_row = lax.broadcasted_iota(jnp.int32, (128, 128), 0) < 64
+
+        def project(q):
+            for j in range(3):
+                o = jnp.dot(abuf[...], wqkv[q, j], preferred_element_type=jnp.float32)
+                o = (o + packs[q, 7:8, j * quarter:(j + 1) * quarter]).astype(jnp.bfloat16)
+                if j == 0:
+                    o = o.astype(jnp.float32) * 0.125
+                    for half in range(per_q):
+                        q_t = o[:, half * 128:(half + 1) * 128].T
+                        qaug[q * per_q + half, :128, :128] = jnp.where(head_row, q_t, 0.0).astype(jnp.bfloat16)
+                        qaug[q * per_q + half, :128, 128:] = jnp.where(head_row, 0.0, q_t).astype(jnp.bfloat16)
+                elif j == 1:
+                    kc[q][tok, :] = o
+                else:
+                    vt[q][:, tok] = o.astype(jnp.float32).T.astype(jnp.bfloat16)
+
         def scores(pair):
-            col = slice(pair * 128, (pair + 1) * 128)
+            col = slice(pair % per_q * 128, (pair % per_q + 1) * 128)
+            kq = kc[pair // per_q]
             top = None
             for b in range(nb):
-                keys = jnp.concatenate([kc[b * KBLK:(b + 1) * KBLK, col], kx[b * KBLK:(b + 1) * KBLK, :]], axis=1)
+                keys = jnp.concatenate([kq[b * KBLK:(b + 1) * KBLK, col], kx[b * KBLK:(b + 1) * KBLK, :]], axis=1)
                 s = jnp.dot(keys, qaug[pair], preferred_element_type=jnp.float32)
                 if b == nb - 1:
                     s = s + diag
@@ -228,27 +308,36 @@
             return top
 
         def weigh(pair, top):
-            col = slice(pair * 128, (pair + 1) * 128)
+            col = slice(pair % per_q * 128, (pair % per_q + 1) * 128)
+            vq = vt[pair // per_q]
             total = None
             acc = None
             for b in range(nb):
                 e = jnp.exp(sbuf[pair % 2, b] - top)
                 part_sum = jnp.sum(e, axis=0, keepdims=True)
                 total = part_sum if total is None else total + part_sum
-                pv = jnp.dot(vt[col, b * KBLK:(b + 1) * KBLK], e.astype(jnp.bfloat16), preferred_element_type=jnp.float32)
+                pv = jnp.dot(vq[col, b * KBLK:(b + 1) * KBLK], e.astype(jnp.bfloat16), preferred_element_type=jnp.float32)
                 acc = pv if acc is None else acc + pv
             acc = acc * (1.0 / total)
             both = jnp.concatenate([acc[:64, :128], acc[64:, 128:]], axis=0)
-            ctx[:, col] = both.T.astype(jnp.bfloat16)
-
-        top = scores(0)
-        for pair in range(pairs):
-            later = scores(pair + 1) if pair + 1 < pairs else None
-            weigh(pair, top)
+            ctx[:, pair * 128:(pair + 1) * 128] = both.T.astype(jnp.bfloat16)
+
+        project(0)
+        top = None
+        for pair in range(pairs + 1):
+            if pair % per_q == 0 and pair // per_q + 1 < tp_n:
+                project(pair // per_q + 1)
+            later = scores(pair) if pair < pairs else None
+            if pair > 0:
+                weigh(pair - 1, top)
             top = later
 
-    r_next = (r + (1 - odd) * sig + tp_n) % tp_n
-    p_next = (p + 2 * odd) % (2 * x_n)
+    more = layer < 2 * x_n - 1
+    nxt = (layer + 1) % (2 * x_n)
+    half_n = nxt // 2
+    x_next = half_n + (1 - nxt % 2) * (1 - half_n % 2) * (2 - 2 * half_n)
+    p_next = 2 * x_next + c
+    r_next = (r + (1 - odd) * (x % 2) * sig + tp_n) % tp_n
 
     def store_unit(v):
         @pl.when(home)
@@ -265,9 +354,25 @@
         def _():
             rcopy(ybuf.at[v], out_at(m, v), db_send.at[v], rr_recv.at[c, v], tp=r_fwd, pp=stage1).start()
 
+    stores = jnp.logical_or(odd == 1, x % 2 == 1)
+
     def unit_step(u, carry):
         tok = pl.ds(pl.multiple_of(u * UNIT, UNIT), UNIT)
 
+        for group, (step0, step1) in (((0, 1), (1, 0)), ((2,), (3, 1)), ((3,), (5, 3))):
+            now = jnp.logical_or(jnp.logical_and(layer == 0, u == min(step0, units - 1)),
+                                 jnp.logical_or(jnp.logical_and(layer == 1, u == min(step1, units - 1)), jnp.logical_and(layer > 1, u == 0)))
+
+            @pl.when(jnp.logical_and(late_source, now))
+            def _():
+                for k in group:
+                    for h in range(2):
+                        relay_weights(k, h)
+
+        @pl.when(jnp.logical_and(relay, u >= lag))
+        def _():
+            relay_unit(u - lag)
+
         @pl.when(layer == 0)
         def _():
             pltpu.make_async_copy(x_hbm.at[m, tok], xbuf.at[u], x0_sem.at[u]).wait()
@@ -286,35 +391,25 @@
             def _():
                 rcopy(xbuf.at[u], out_at(m, u), fa_send.at[u], o_recv, pp=partner).start()
 
-            rcopy(xbuf.at[u], out_at(m, u), fb_send.at[u], o_recv, tp=r_fwd, pp=stage0).start()
-
-        @pl.when(u > 0)
+            @pl.when(x % 2 == 1)
+            def _():
+                rcopy(xbuf.at[u], out_at(m, u), fb_send.at[u], o_recv, tp=r_fwd, pp=stage0).start()
+
+            @pl.when(x % 2 == 0)
+            def _():
+                rcopy(xbuf.at[u], out_at(m, u), fb_send.at[u], rr_recv.at[c, u], tp=r_fwd, pp=stage0).start()
+                rcopy(xbuf.at[u], out_at(m, u), fc_send.at[u], o_recv, tp=r_bwd, pp=stage0).start()
+
+        @pl.when(jnp.logical_and(stores, u > 0))
         def _():
             store_unit(u - 1)
 
         xin = xbuf[u].astype(jnp.float32)
         abuf[...] = layer_norm(xin, packs[0, 0:1, :], packs[0, 1:2, :])
-        head_row = lax.broadcasted_iota(jnp.int32, (128, 128), 0) < 64
-        for q in range(tp_n):
-            for j in range(3):
-                o = jnp.dot(abuf[...], wqkv[q, j], preferred_element_type=jnp.float32)
-                o = (o + packs[q, 7:8, j * quarter:(j + 1) * quarter]).astype(jnp.bfloat16)
-                if j == 0:
-                    o = o.astype(jnp.float32) * 0.125
-                    for half in range(quarter // 128):
-                        q_t = o[:, half * 128:(half + 1) * 128].T
-                        pair = q * (quarter // 128) + half
-                        qaug[pair, :128, :128] = jnp.where(head_row, q_t, 0.0).astype(jnp.bfloat16)
-                        qaug[pair, :128, 128:] = jnp.where(head_row, 0.0, q_t).astype(jnp.bfloat16)
-                elif j == 1:
-                    kc[tok, q * quarter:(q + 1) * quarter] = o
-                else:
-                    vt[q * quarter:(q + 1) * quarter, tok] = o.astype(jnp.float32).T.astype(jnp.bfloat16)
-
         for nb in range(1, seq // KBLK + 1):
             @pl.when(u // 2 + 1 == nb)
             def _():
-                attention(nb, cmask[u % 2])
+                attention(nb, cmask[u % 2], tok)
 
         for n in range(model // quarter):
             cols = slice(n * quarter, (n + 1) * quarter)
@@ -332,61 +427,57 @@
             cols = slice(n * half_model, (n + 1) * half_model)
             down = jnp.dot(ubuf[...], wdn[:, cols], preferred_element_type=jnp.float32)
             ybuf[u, :, cols] = (hbuf[:, cols].astype(jnp.float32) + down + packs[0, 5:6, cols]).astype(jnp.bfloat16)
-            rcopy(ybuf.at[u, :, cols], xbuf.at[u, :, cols], s_send.at[u], x_recv.at[u], tp=r_next, pp=p_next).start()
-
-        @pl.when(jnp.logical_and(relay, u >= LAG))
-        def _():
-            relay_unit(u - LAG)
+
+            @pl.when(more)
+            def _():
+                rcopy(ybuf.at[u, :, cols], xbuf.at[u, :, cols], s_send.at[u], x_recv.at[u], tp=r_next, pp=p_next).start()
 
         return carry
 
     lax.fori_loop(0, units, unit_step, 0)
-    store_unit(units - 1)
+
+    @pl.when(stores)
+    def _():
+        store_unit(units - 1)
 
     @pl.when(relay)
     def _():
-        for v in range(max(0, units - LAG), units):
+        def rest(v, carry):
             relay_unit(v)
-
-    def sent(view, sem):
-        rcopy(view, view, sem, sem, pp=partner).wait_send()
+            return carry
+
+        lax.fori_loop(units - lag, units, rest, 0)
+
+    @pl.when(moved)
+    def _():
+        for k, h in pieces:
+            sent(sw(k, h), sw_send.at[k, h])
 
     @pl.when(home)
     def _():
-        sent(wsrc(4), pk_send.at[0])
-        for k in range(4):
-            sent(rl(k, 0), rl_send.at[0, k])
-            sent(rl(k, 1), rl_send.at[1, k])
-        for k in range(5):
-            sent(wsrc(k), fwd_send.at[k])
-        idx = 5
-        for k in (4, 0, 1, 2, 3):
-            for d in range(2):
-                sent(wsrc(k), fwd_send.at[idx])
-                idx += 1
-        sent(wsrc(4), fwd_send.at[idx])
-        idx += 1
-        for k in range(4):
-            for h in range(2):
-                sent(wsrc(k, h), fwd_send.at[idx])
-                idx += 1
-
-    @pl.when(jnp.logical_not(home))
-    def _():
-        for k in range(5):
-            for d in range(2):
-                sent(wsrc(k), dir_send.at[d, k])
-        for k in range(4):
-            for d in range(2):
-                sent(rl(k, d), rl_send.at[d, k])
+        sent(sw_pack, pk_send.at[0])
+        for k, h in mats:
+            sent(rl(k, h), rl_send.at[h, k])
+        for d in range(4):
+            for k, h in pieces:
+                sent(sw(k, h), fwd_send.at[d, k, h])
+
+    @pl.when(late_source)
+    def _():
+        handed_out()
 
     def drain(u, carry):
-        sent(ybuf.at[u], s_send.at[u])
-        sent(ybuf.at[u], da_send.at[u])
-
-        @pl.when(jnp.logical_not(home))
-        def _():
-            sent(ybuf.at[u], od_send.at[u])
+        @pl.when(more)
+        def _():
+            sent(ybuf.at[u], s_send.at[u])
+
+        @pl.when(stores)
+        def _():
+            sent(ybuf.at[u], da_send.at[u])
+
+            @pl.when(jnp.logical_not(home))
+            def _():
+                sent(ybuf.at[u], od_send.at[u])
 
         @pl.when(relay)
         def _():
@@ -398,13 +489,13 @@
             sent(ybuf.at[u], db_send.at[u])
             sent(ybuf.at[u], fb_send.at[u])
 
+            @pl.when(x % 2 == 0)
+            def _():
+                sent(ybuf.at[u], fc_send.at[u])
+
             @pl.when(c == 1)
             def _():
                 sent(ybuf.at[u], fa_send.at[u])
-
-        @pl.when(layer == 0)
-        def _():
-            wwait(xbuf.at[u], x_recv.at[u])
 
         return carry
 
@@ -452,10 +543,15 @@
                 pltpu.VMEM((2, quarter // 2, model_n), bf16),
                 pltpu.VMEM((2, model_n // 2, hid_q), bf16),
                 pltpu.VMEM((2, hid_q // 2, model_n), bf16),
+                pltpu.VMEM((3, model_n, quarter), bf16),
+                pltpu.VMEM((quarter, model_n), bf16),
+                pltpu.VMEM((model_n, hid_q), bf16),
+                pltpu.VMEM((hid_q, model_n), bf16),
+                pltpu.VMEM(pack.shape, f32),
                 pltpu.VMEM((units, UNIT, model_n), bf16),
                 pltpu.VMEM((units, UNIT, model_n), bf16),
-                pltpu.VMEM((seq_n, model_n), bf16),
-                pltpu.VMEM((model_n, seq_n), bf16),
+                *[pltpu.VMEM((seq_n, quarter), bf16)] * tp_size,
+                *[pltpu.VMEM((quarter, seq_n), bf16)] * tp_size,
                 pltpu.VMEM((seq_n, 128), bf16),
                 pltpu.VMEM((pairs, 256, 256), bf16),
                 pltpu.VMEM((2, KBLK, 256), f32),
@@ -464,8 +560,8 @@
                 pltpu.VMEM((UNIT, model_n), bf16),
                 pltpu.VMEM((UNIT, model_n), bf16),
                 pltpu.VMEM((UNIT, tp_size * hid_q), bf16),
-                dma((5,)), dma((4, 5, 2)), dma((24,)), dma((2, 4)), dma((2, 4)), dma((2, 5)), dma((1,)),
-                dma((units,)), dma((units,)), dma((units,)), dma((units,)), dma((units,)), dma((units,)), dma((units,)), dma((units,)),
+                dma((5, 2)), dma((5, 2)), dma((4, 5, 2)), dma((4, 5, 2)), dma((2, 4)), dma((2, 4)), dma((2, 5, 2)), dma((1,)), pltpu.SemaphoreType.REGULAR,
+                *[dma((units,))] * 9,
                 dma((2, units)), dma((2, units)), dma,
             ],
             compiler_params=pltpu.CompilerParams(collective_id=0, has_side_effects=True, vmem_limit_bytes=63 * 1024 * 1024),

time: 322 us -> 404 us (1.25)
  Pallas kernels: 312 us -> 393 us
    pallas_call x1, Pallas kernels: 312 us -> 393 us  [per_device(): pl.pallas_call(functools.partial(kernel, heads_n), out_shape=jax.ShapeDty...]
where the time goes in v3:
time: 404 us
  Pallas kernels  393 us (97%)
  local copies, waits for them, and re-layouts  9.38 us (2%)
    pallas_call x1, Pallas kernels, per_device(): pl.pallas_call(functools.partial(kernel, heads_n), out_shape=jax.ShapeDty...  393 us

profile of v3, /device:TPU:103, one launch (start us, length us, event | category | flops | bytes accessed | tf_op | source)
XLA Modules:
  0.0 403.5 jit_solution(4648904128026259519)
XLA Ops:
  0.0 0.8 reshape.14
  0.8 0.8 concatenate.3
  1.6 0.6 convert_element_type.5.pack_in
  2.2 393.5 %shard_map.136 = bf16[4,1024,1024]{2,1,0:T(8,128)(2,1)} custom-call(bf16[4,1024,1024]{2,1,0:T(8,128)(2,1)} %bitcast.12, s32[4]{0:T(128)} %bitcast.17, bf16[3,1024,256]{2,1,0:T(8,128)(2,1)} %bitcast.15, bf16[256,1024]{1,0:T(8,128)(2,1)} %bitcast.16, bf16[1024,1024]{1,0:T(8,128)(2,1)} %bitcast.13, bf16[1024,1024]{1,0:T(8,128)(2,1)} %bitcast.14, ...), custom_call_target="tpu_custom_call" | custom-call | flops 30000001024 | bytes 40000000 | tf_op jit(solution)/shard_map/pallas_call | solution.py:531
  395.7 7.8 %copy.17 = bf16[1,4,1,1024,1024]{4,3,2,1,0:T(8,128)(2,1)} copy(bf16[1,4,1,1024,1024]{4,3,2,1,0:T(8,128)(2,1)} %bitcast.11) | data formatting | bytes 16777216
  (1 shorter events, 0.0 us)

commit v4 on v3

--- a/solution.py
+++ b/solution.py
@@ -257,8 +257,8 @@
 
     @pl.when(late_source)
     def _():
+        hand_out()
         from_partner()
-        hand_out()
 
     def out_at(mm, u):
         return out.at[mm, pl.ds(pl.multiple_of(u * UNIT, UNIT), UNIT)]

time: 404 us -> 334 us (0.83)
  Pallas kernels: 393 us -> 323 us
    pallas_call x1, Pallas kernels: 393 us -> 323 us  [per_device(): pl.pallas_call(functools.partial(kernel, heads_n), out_shape=jax.ShapeDty...]
where the time goes in v4:
time: 334 us; the launch traced here: 333 us
  Pallas kernels  323 us (97%)
  local copies, waits for them, and re-layouts  9.38 us (3%)
    pallas_call x1, Pallas kernels, per_device(): pl.pallas_call(functools.partial(kernel, heads_n), out_shape=jax.ShapeDty...  323 us
    unnamed x1, local copies, waits for them, and re-layouts  7.76 us

profile of v4, /device:TPU:103, one launch (start us, length us, event | category | flops | bytes accessed | tf_op | source)
XLA Modules:
  0.0 333.4 jit_solution(13321437754679627995)
XLA Ops:
  0.0 0.8 reshape.14
  0.8 0.8 concatenate.3
  1.6 0.6 convert_element_type.5.pack_in
  2.2 323.4 %shard_map.136 = bf16[4,1024,1024]{2,1,0:T(8,128)(2,1)} custom-call(bf16[4,1024,1024]{2,1,0:T(8,128)(2,1)} %bitcast.12, s32[4]{0:T(128)} %bitcast.17, bf16[3,1024,256]{2,1,0:T(8,128)(2,1)} %bitcast.15, bf16[256,1024]{1,0:T(8,128)(2,1)} %bitcast.16, bf16[1024,1024]{1,0:T(8,128)(2,1)} %bitcast.13, bf16[1024,1024]{1,0:T(8,128)(2,1)} %bitcast.14, ...), custom_call_target="tpu_custom_call" | custom-call | flops 30000001024 | bytes 40000000 | tf_op jit(solution)/shard_map/pallas_call | solution.py:531
  325.7 7.8 %copy.17 = bf16[1,4,1,1024,1024]{4,3,2,1,0:T(8,128)(2,1)} copy(bf16[1,4,1,1024,1024]{4,3,2,1,0:T(8,128)(2,1)} %bitcast.11) | data formatting | bytes 16777216
  (1 shorter events, 0.0 us)

commit v5 on v4

--- a/solution.py
+++ b/solution.py
@@ -266,7 +266,8 @@
     m_a = micro_of(rm, 0, stage1)
     m_b = micro_of(rp, 1, stage1)
     relay = jnp.logical_and(odd == 0, jnp.logical_or(c == 1, x % 2 == 0))
-    lag = min(5, units) * (x % 2) + units * ((x // 2) * (1 - x % 2))
+    lag = min(5, units) * (x % 2) + (1 - x % 2) * (min(5, units) + (units - min(5, units)) * (x // 2))
+    hold = min(4, units) * (1 - (x + 2) // 3) + (x + 2) // 3
 
     def relay_unit(v):
         wwait(out_at(m_a, v), rr_recv.at[0, v])
@@ -340,6 +341,25 @@
     r_next = (r + (1 - odd) * (x % 2) * sig + tp_n) % tp_n
 
     def store_unit(v):
+        @pl.when(odd == 1)
+        def _():
+            @pl.when(c == 0)
+            def _():
+                pltpu.make_async_copy(xbuf.at[v], out_at(m, v), o_recv).start()
+
+            @pl.when(c == 1)
+            def _():
+                rcopy(xbuf.at[v], out_at(m, v), fa_send.at[v], o_recv, pp=partner).start()
+
+            @pl.when(x % 2 == 1)
+            def _():
+                rcopy(xbuf.at[v], out_at(m, v), fb_send.at[v], o_recv, tp=r_fwd, pp=stage0).start()
+
+            @pl.when(x % 2 == 0)
+            def _():
+                rcopy(xbuf.at[v], out_at(m, v), fb_send.at[v], rr_recv.at[c, v], tp=r_fwd, pp=stage0).start()
+                rcopy(xbuf.at[v], out_at(m, v), fc_send.at[v], o_recv, tp=r_bwd, pp=stage0).start()
+
         @pl.when(home)
         def _():
             pltpu.make_async_copy(ybuf.at[v], out_at(m, v), o_recv).start()
@@ -381,28 +401,9 @@
         def _():
             wwait(xbuf.at[u], x_recv.at[u])
 
-        @pl.when(odd == 1)
-        def _():
-            @pl.when(c == 0)
-            def _():
-                pltpu.make_async_copy(xbuf.at[u], out_at(m, u), o_recv).start()
-
-            @pl.when(c == 1)
-            def _():
-                rcopy(xbuf.at[u], out_at(m, u), fa_send.at[u], o_recv, pp=partner).start()
-
-            @pl.when(x % 2 == 1)
-            def _():
-                rcopy(xbuf.at[u], out_at(m, u), fb_send.at[u], o_recv, tp=r_fwd, pp=stage0).start()
-
-            @pl.when(x % 2 == 0)
-            def _():
-                rcopy(xbuf.at[u], out_at(m, u), fb_send.at[u], rr_recv.at[c, u], tp=r_fwd, pp=stage0).start()
-                rcopy(xbuf.at[u], out_at(m, u), fc_send.at[u], o_recv, tp=r_bwd, pp=stage0).start()
-
-        @pl.when(jnp.logical_and(stores, u > 0))
-        def _():
-            store_unit(u - 1)
+        @pl.when(jnp.logical_and(stores, u >= hold))
+        def _():
+            store_unit(u - hold)
 
         xin = xbuf[u].astype(jnp.float32)
         abuf[...] = layer_norm(xin, packs[0, 0:1, :], packs[0, 1:2, :])
@@ -438,7 +439,11 @@
 
     @pl.when(stores)
     def _():
-        store_unit(units - 1)
+        def last(v, carry):
+            store_unit(v)
+            return carry
+
+        lax.fori_loop(units - hold, units, last, 0)
 
     @pl.when(relay)
     def _():

time: 334 us -> 307 us (0.919)
  Pallas kernels: 323 us -> 297 us
    pallas_call x1, Pallas kernels: 323 us -> 297 us  [per_device(): pl.pallas_call(functools.partial(kernel, heads_n), out_shape=jax.ShapeDty...]
where the time goes in v5:
time: 307 us
  Pallas kernels  297 us (97%)
  local copies, waits for them, and re-layouts  9.38 us (3%)
    pallas_call x1, Pallas kernels, per_device(): pl.pallas_call(functools.partial(kernel, heads_n), out_shape=jax.ShapeDty...  297 us
    unnamed x1, local copies, waits for them, and re-layouts  7.76 us

profile of v5, /device:TPU:103, one launch (start us, length us, event | category | flops | bytes accessed | tf_op | source)
XLA Modules:
  0.0 306.9 jit_solution(3576741777964795988)
XLA Ops:
  0.0 0.8 reshape.14
  0.8 0.8 concatenate.3
  1.6 0.6 convert_element_type.5.pack_in
  2.2 296.9 %shard_map.136 = bf16[4,1024,1024]{2,1,0:T(8,128)(2,1)} custom-call(bf16[4,1024,1024]{2,1,0:T(8,128)(2,1)} %bitcast.12, s32[4]{0:T(128)} %bitcast.17, bf16[3,1024,256]{2,1,0:T(8,128)(2,1)} %bitcast.15, bf16[256,1024]{1,0:T(8,128)(2,1)} %bitcast.16, bf16[1024,1024]{1,0:T(8,128)(2,1)} %bitcast.13, bf16[1024,1024]{1,0:T(8,128)(2,1)} %bitcast.14, ...), custom_call_target="tpu_custom_call" | custom-call | flops 30000001024 | bytes 40000000 | tf_op jit(solution)/shard_map/pallas_call | solution.py:536
  299.2 7.8 %copy.17 = bf16[1,4,1,1024,1024]{4,3,2,1,0:T(8,128)(2,1)} copy(bf16[1,4,1,1024,1024]{4,3,2,1,0:T(8,128)(2,1)} %bitcast.11) | data formatting | bytes 16777216
  (1 shorter events, 0.0 us)

commit v6 on v5

--- a/solution.py
+++ b/solution.py
@@ -193,11 +193,13 @@
     def to_partner(k, q, d, h):
         rcopy(wdst(k, q, h), wdst(k, q, h), fwd_send.at[d, k, h], w_recv.at[d, k, h], pp=partner).start()
 
-    def hand_out():
-        for k, h in pieces:
+    def hand_out(behind=()):
+        for i, (k, h) in enumerate(pieces):
             wwait(sw(k, h), sw_recv.at[k, h])
             rcopy(sw(k, h), wdst(k, r, h), dir_send.at[0, k, h], w_recv.at[3, k, h], tp=rp).start()
             rcopy(sw(k, h), wdst(k, r, h), dir_send.at[1, k, h], w_recv.at[1, k, h], tp=rm).start()
+            if 3 <= i < len(behind) + 3:
+                relay_weights(*behind[i - 3])
 
     def relay_weights(k, h):
         wwait(rl(k, h), rl_recv.at[h, k])
@@ -248,8 +250,8 @@
 
     @pl.when(jnp.logical_not(jnp.logical_or(home, early_row)))
     def _():
-        hand_out()
-        for k, h in mats:
+        hand_out(mats)
+        for k, h in mats[len(pieces) - 3:]:
             relay_weights(k, h)
         handed_out()
         pl.semaphore_signal(go, inc=1, device_id={"pp": partner}, device_id_type=MESH)
@@ -340,7 +342,7 @@
     p_next = 2 * x_next + c
     r_next = (r + (1 - odd) * (x % 2) * sig + tp_n) % tp_n
 
-    def store_unit(v):
+    def store_input(v):
         @pl.when(odd == 1)
         def _():
             @pl.when(c == 0)
@@ -360,6 +362,7 @@
                 rcopy(xbuf.at[v], out_at(m, v), fb_send.at[v], rr_recv.at[c, v], tp=r_fwd, pp=stage0).start()
                 rcopy(xbuf.at[v], out_at(m, v), fc_send.at[v], o_recv, tp=r_bwd, pp=stage0).start()
 
+    def store_unit(v):
         @pl.when(home)
         def _():
             pltpu.make_async_copy(ybuf.at[v], out_at(m, v), o_recv).start()
@@ -379,7 +382,7 @@
     def unit_step(u, carry):
         tok = pl.ds(pl.multiple_of(u * UNIT, UNIT), UNIT)
 
-        for group, (step0, step1) in (((0, 1), (1, 0)), ((2,), (3, 1)), ((3,), (5, 3))):
+        for group, (step0, step1) in (((0, 1), (2, 0)), ((2,), (4, 1)), ((3,), (6, 3))):
             now = jnp.logical_or(jnp.logical_and(layer == 0, u == min(step0, units - 1)),
                                  jnp.logical_or(jnp.logical_and(layer == 1, u == min(step1, units - 1)), jnp.logical_and(layer > 1, u == 0)))
 
@@ -400,6 +403,10 @@
         @pl.when(layer > 0)
         def _():
             wwait(xbuf.at[u], x_recv.at[u])
+
+        @pl.when(jnp.logical_and(stores, u >= hold - 1))
+        def _():
+            store_input(u - hold + 1)
 
         @pl.when(jnp.logical_and(stores, u >= hold))
         def _():
@@ -444,6 +451,12 @@
             return carry
 
         lax.fori_loop(units - hold, units, last, 0)
+
+        def last_input(v, carry):
+            store_input(v)
+            return carry
+
+        lax.fori_loop(units - hold + 1, units, last_input, 0)
 
     @pl.when(relay)
     def _():

time: 307 us -> 305 us (level)
  no operation moved by 1% of the time
where the time goes in v6:
time: 305 us
  Pallas kernels  295 us (97%)
  local copies, waits for them, and re-layouts  9.38 us (3%)
    pallas_call x1, Pallas kernels, per_device(): pl.pallas_call(functools.partial(kernel, heads_n), out_shape=jax.ShapeDty...  295 us
    unnamed x1, local copies, waits for them, and re-layouts  7.76 us

profile of v6, /device:TPU:103, one launch (start us, length us, event | category | flops | bytes accessed | tf_op | source)
XLA Modules:
  0.0 305.1 jit_solution(1265244939854891774)
XLA Ops:
  0.0 0.8 reshape.14
  0.8 0.8 concatenate.3
  1.6 0.6 convert_element_type.5.pack_in
  2.2 295.1 %shard_map.136 = bf16[4,1024,1024]{2,1,0:T(8,128)(2,1)} custom-call(bf16[4,1024,1024]{2,1,0:T(8,128)(2,1)} %bitcast.12, s32[4]{0:T(128)} %bitcast.17, bf16[3,1024,256]{2,1,0:T(8,128)(2,1)} %bitcast.15, bf16[256,1024]{1,0:T(8,128)(2,1)} %bitcast.16, bf16[1024,1024]{1,0:T(8,128)(2,1)} %bitcast.13, bf16[1024,1024]{1,0:T(8,128)(2,1)} %bitcast.14, ...), custom_call_target="tpu_custom_call" | custom-call | flops 30000001024 | bytes 40000000 | tf_op jit(solution)/shard_map/pallas_call | solution.py:549
  297.3 7.8 %copy.17 = bf16[1,4,1,1024,1024]{4,3,2,1,0:T(8,128)(2,1)} copy(bf16[1,4,1,1024,1024]{4,3,2,1,0:T(8,128)(2,1)} %bitcast.11) | data formatting | bytes 16777216
  (1 shorter events, 0.0 us)

commit v7 on v6

--- a/solution.py
+++ b/solution.py
@@ -69,7 +69,8 @@
     layer = odd * (2 * x + 1) + (1 - odd) * 2 * even_col
     home = odd == c
     moved = jnp.logical_and(c == 0, x % 2 == 0)
-    early_row = r % 2 == 0
+    level = x == 1
+    ahead = jnp.logical_or(r % 2 == 0, level)
     rp, rm, ro = (r + 1) % tp_n, (r + 3) % tp_n, (r + 2) % tp_n
     partner = 2 * x + (1 - c)
     sig = 1 - 2 * c
@@ -227,12 +228,12 @@
             if k == 4:
                 rcopy(wdst(k, r), wdst(k, r), pk_send.at[0], w_recv.at[2, k, h], tp=ro).start()
             else:
-                @pl.when(early_row)
+                @pl.when(ahead)
                 def _():
                     to_relay(k, h)
             to_partner(k, r, 0, h)
 
-        @pl.when(jnp.logical_not(early_row))
+        @pl.when(jnp.logical_not(ahead))
         def _():
             pl.semaphore_wait(go, 1)
             for k, h in mats:
@@ -246,15 +247,19 @@
             wwait(wdst(k, ro, h), w_recv.at[2, k, h])
             to_partner(k, ro, 2, h)
 
-    late_source = jnp.logical_and(early_row, jnp.logical_not(home))
-
-    @pl.when(jnp.logical_not(jnp.logical_or(home, early_row)))
+    late_source = jnp.logical_not(jnp.logical_or(home, jnp.logical_or(r % 2 == 1, level)))
+
+    @pl.when(jnp.logical_not(jnp.logical_or(home, late_source)))
     def _():
         hand_out(mats)
         for k, h in mats[len(pieces) - 3:]:
             relay_weights(k, h)
         handed_out()
-        pl.semaphore_signal(go, inc=1, device_id={"pp": partner}, device_id_type=MESH)
+
+        @pl.when(jnp.logical_not(level))
+        def _():
+            pl.semaphore_signal(go, inc=1, device_id={"pp": partner}, device_id_type=MESH)
+
         from_partner()
 
     @pl.when(late_source)
@@ -382,7 +387,7 @@
     def unit_step(u, carry):
         tok = pl.ds(pl.multiple_of(u * UNIT, UNIT), UNIT)
 
-        for group, (step0, step1) in (((0, 1), (2, 0)), ((2,), (4, 1)), ((3,), (6, 3))):
+        for group, (step0, step1) in (((0, 1), (3, 1)), ((2,), (5, 3)), ((3,), (7, 4))):
             now = jnp.logical_or(jnp.logical_and(layer == 0, u == min(step0, units - 1)),
                                  jnp.logical_or(jnp.logical_and(layer == 1, u == min(step1, units - 1)), jnp.logical_and(layer > 1, u == 0)))
 

time: 305 us -> 331 us (1.085)
  Pallas kernels: 295 us -> 320 us
    pallas_call x1, Pallas kernels: 295 us -> 320 us  [per_device(): pl.pallas_call(functools.partial(kernel, heads_n), out_shape=jax.ShapeDty...]
where the time goes in v7:
time: 331 us; the launch traced here: 330 us
  Pallas kernels  320 us (97%)
  local copies, waits for them, and re-layouts  9.38 us (3%)
    pallas_call x1, Pallas kernels, per_device(): pl.pallas_call(functools.partial(kernel, heads_n), out_shape=jax.ShapeDty...  320 us
    unnamed x1, local copies, waits for them, and re-layouts  7.76 us

profile of v7, /device:TPU:103, one launch (start us, length us, event | category | flops | bytes accessed | tf_op | source)
XLA Modules:
  0.0 330.4 jit_solution(15202092784943799374)
XLA Ops:
  0.0 0.8 reshape.14
  0.8 0.8 concatenate.3
  1.6 0.6 convert_element_type.5.pack_in
  2.2 320.4 %shard_map.136 = bf16[4,1024,1024]{2,1,0:T(8,128)(2,1)} custom-call(bf16[4,1024,1024]{2,1,0:T(8,128)(2,1)} %bitcast.12, s32[4]{0:T(128)} %bitcast.17, bf16[3,1024,256]{2,1,0:T(8,128)(2,1)} %bitcast.15, bf16[256,1024]{1,0:T(8,128)(2,1)} %bitcast.16, bf16[1024,1024]{1,0:T(8,128)(2,1)} %bitcast.13, bf16[1024,1024]{1,0:T(8,128)(2,1)} %bitcast.14, ...), custom_call_target="tpu_custom_call" | custom-call | flops 30000001024 | bytes 40000000 | tf_op jit(solution)/shard_map/pallas_call | solution.py:554
  322.6 7.8 %copy.17 = bf16[1,4,1,1024,1024]{4,3,2,1,0:T(8,128)(2,1)} copy(bf16[1,4,1,1024,1024]{4,3,2,1,0:T(8,128)(2,1)} %bitcast.11) | data formatting | bytes 16777216
  (1 shorter events, 0.0 us)

commit v8 on v7

--- a/solution.py
+++ b/solution.py
@@ -274,7 +274,7 @@
     m_b = micro_of(rp, 1, stage1)
     relay = jnp.logical_and(odd == 0, jnp.logical_or(c == 1, x % 2 == 0))
     lag = min(5, units) * (x % 2) + (1 - x % 2) * (min(5, units) + (units - min(5, units)) * (x // 2))
-    hold = min(4, units) * (1 - (x + 2) // 3) + (x + 2) // 3
+    hold = min(5, units) * (1 - (x + 2) // 3) + (x + 2) // 3
 
     def relay_unit(v):
         wwait(out_at(m_a, v), rr_recv.at[0, v])
@@ -387,7 +387,7 @@
     def unit_step(u, carry):
         tok = pl.ds(pl.multiple_of(u * UNIT, UNIT), UNIT)
 
-        for group, (step0, step1) in (((0, 1), (3, 1)), ((2,), (5, 3)), ((3,), (7, 4))):
+        for group, (step0, step1) in (((0, 1), (2, 0)), ((2,), (4, 1)), ((3,), (6, 2))):
             now = jnp.logical_or(jnp.logical_and(layer == 0, u == min(step0, units - 1)),
                                  jnp.logical_or(jnp.logical_and(layer == 1, u == min(step1, units - 1)), jnp.logical_and(layer > 1, u == 0)))
 

time: 331 us -> 299 us (0.903)
  Pallas kernels: 320 us -> 289 us
    pallas_call x1, Pallas kernels: 320 us -> 289 us  [per_device(): pl.pallas_call(functools.partial(kernel, heads_n), out_shape=jax.ShapeDty...]
where the time goes in v8:
time: 299 us
  Pallas kernels  289 us (97%)
  local copies, waits for them, and re-layouts  9.38 us (3%)
    pallas_call x1, Pallas kernels, per_device(): pl.pallas_call(functools.partial(kernel, heads_n), out_shape=jax.ShapeDty...  289 us
    unnamed x1, local copies, waits for them, and re-layouts  7.76 us

profile of v8, /device:TPU:103, one launch (start us, length us, event | category | flops | bytes accessed | tf_op | source)
XLA Modules:
  0.0 298.9 jit_solution(5746332650166288623)
XLA Ops:
  0.0 0.8 reshape.14
  0.8 0.8 concatenate.3
  1.6 0.6 convert_element_type.5.pack_in
  2.2 288.8 %shard_map.136 = bf16[4,1024,1024]{2,1,0:T(8,128)(2,1)} custom-call(bf16[4,1024,1024]{2,1,0:T(8,128)(2,1)} %bitcast.12, s32[4]{0:T(128)} %bitcast.17, bf16[3,1024,256]{2,1,0:T(8,128)(2,1)} %bitcast.15, bf16[256,1024]{1,0:T(8,128)(2,1)} %bitcast.16, bf16[1024,1024]{1,0:T(8,128)(2,1)} %bitcast.13, bf16[1024,1024]{1,0:T(8,128)(2,1)} %bitcast.14, ...), custom_call_target="tpu_custom_call" | custom-call | flops 30000001024 | bytes 40000000 | tf_op jit(solution)/shard_map/pallas_call | solution.py:554
  291.1 7.8 %copy.17 = bf16[1,4,1,1024,1024]{4,3,2,1,0:T(8,128)(2,1)} copy(bf16[1,4,1,1024,1024]{4,3,2,1,0:T(8,128)(2,1)} %bitcast.11) | data formatting | bytes 16777216
  (1 shorter events, 0.0 us)

commit v9 on v8

--- a/solution.py
+++ b/solution.py
@@ -56,9 +56,10 @@
     units = xbuf.shape[0]
     model = xbuf.shape[2]
     seq = units * UNIT
-    quarter = wqkv.shape[3]
-    hid_q = wup.shape[2]
+    quarter = wqkv.shape[1] // 3 * 128
+    hid_q = wup.shape[1] * 128
     pairs = model // 128
+    per_q = quarter // 128
 
     r = lax.axis_index("tp")
     p = lax.axis_index("pp")
@@ -98,29 +99,20 @@
         pl.semaphore_signal(barrier, inc=1, device_id={"pp": 2 * ((x + dx) % x_n) + c}, device_id_type=MESH)
     pl.semaphore_wait(barrier, 10)
 
-    def wsrc(k, h=None):
-        if k == 4:
-            return pack_in
+    def wsrc(k, h, n):
         if k == 0:
-            return wqkv_in if h is None else wqkv_in.at[:, pl.ds(h * (model // 2), model // 2), :]
+            return wqkv_in.at[n // per_q, pl.ds(h * (model // 2), model // 2), pl.ds(n % per_q * 128, 128)]
         ref = (None, wout_in, wup_in, wdn_in)[k]
-        if h is None:
-            return ref
         half = ref.shape[0] // 2
-        return ref.at[pl.ds(h * half, half)]
-
-    def wdst(k, q, h=None):
-        if k == 0:
-            return wqkv.at[q] if h is None else wqkv.at[q, :, pl.ds(h * (model // 2), model // 2), :]
-        if k == 2:
-            return wup.at[q] if h is None else wup.at[q, pl.ds(h * (model // 2), model // 2)]
+        return ref.at[pl.ds(h * half, half), pl.ds(n * 128, 128)]
+
+    def wdst(k, q, h=0):
         if k == 4:
             return packs.at[q]
-        ref, rows = (wout, quarter) if k == 1 else (wdn, hid_q)
-        if h is None:
-            return ref.at[pl.ds(pl.multiple_of(q * rows, rows), rows)]
-        half = rows // 2
-        return ref.at[pl.ds(pl.multiple_of(q * rows + h * half, half), half)]
+        if k == 0 or k == 2:
+            return (wqkv, None, wup)[k].at[q, :, pl.ds(h * (model // 2), model // 2), :]
+        ref, half = (wout, quarter // 2) if k == 1 else (wdn, hid_q // 2)
+        return ref.at[:, pl.ds(pl.multiple_of((2 * q + h) * half, half), half), :]
 
     def rl(k, h):
         return (rl_qkv, rl_out, rl_up, rl_dn)[k].at[h]
@@ -128,11 +120,20 @@
     def sw(k, h):
         if k == 4:
             return sw_pack
-        if k == 0:
-            return sw_qkv.at[:, pl.ds(h * (model // 2), model // 2), :]
-        ref = (None, sw_out, sw_up, sw_dn)[k]
-        half = ref.shape[0] // 2
-        return ref.at[pl.ds(h * half, half)]
+        ref = (sw_qkv, sw_out, sw_up, sw_dn)[k]
+        half = ref.shape[1] // 2
+        return ref.at[:, pl.ds(h * half, half), :]
+
+    def fetch(k, h, dst, move):
+        if k == 4:
+            todo = [(pack_in, dst)]
+        else:
+            todo = [(wsrc(k, h, n), dst.at[n]) for n in range(dst.shape[0])]
+        for src, to in todo:
+            if move:
+                rcopy(src, to, sw_send.at[k, h], sw_recv.at[k, h], pp=2 * (2 - x)).start()
+            else:
+                pltpu.make_async_copy(src, to, sw_recv.at[k, h]).start()
 
     def wwait(view, sem):
         rcopy(view, view, sem, sem, pp=partner).wait_recv()
@@ -143,22 +144,22 @@
     @pl.when(jnp.logical_and(moved, odd == 1))
     def _():
         for k, h in pieces:
-            rcopy(wsrc(k, h), wdst(k, r, h), sw_send.at[k, h], sw_recv.at[k, h], pp=2 * (2 - x)).start()
+            fetch(k, h, wdst(k, r, h), True)
 
     @pl.when(jnp.logical_and(moved, odd == 0))
     def _():
         for k, h in pieces:
-            rcopy(wsrc(k, h), sw(k, h), sw_send.at[k, h], sw_recv.at[k, h], pp=2 * (2 - x)).start()
+            fetch(k, h, sw(k, h), True)
 
     @pl.when(jnp.logical_and(jnp.logical_not(moved), home))
     def _():
         for k, h in pieces:
-            pltpu.make_async_copy(wsrc(k, h), wdst(k, r, h), sw_recv.at[k, h]).start()
+            fetch(k, h, wdst(k, r, h), False)
 
     @pl.when(jnp.logical_not(jnp.logical_or(moved, home)))
     def _():
         for k, h in pieces:
-            pltpu.make_async_copy(wsrc(k, h), sw(k, h), sw_recv.at[k, h]).start()
+            fetch(k, h, sw(k, h), False)
 
     @pl.when(layer == 0)
     def _():
@@ -182,7 +183,8 @@
         (h0, m0, l0), (h1, m1, l1) = split_bf16(slopes[2 * pair]), split_bf16(slopes[2 * pair + 1])
         hi, mid, low = jnp.where(second, h1, h0), jnp.where(second, m1, m0), jnp.where(second, l1, l0)
         val = jnp.where(row < 2, hi, jnp.where(row < 4, mid, jnp.where(row < 6, low, jnp.where(row == 6, 1.0, 0.0))))
-        qaug[pair, 128:, :] = val.astype(jnp.bfloat16)
+        for side in range(2):
+            qaug[pair, side, 128:, :] = val[:, side * 128:(side + 1) * 128].astype(jnp.bfloat16)
     kpos = lax.broadcasted_iota(jnp.int32, (KBLK, 256), 0)
     qpos = lax.broadcasted_iota(jnp.int32, (KBLK, 256), 1) % 128
     cmask[0] = jnp.where(kpos <= qpos, 0.0, NEG)
@@ -282,32 +284,42 @@
         wwait(out_at(m_b, v), rr_recv.at[1, v])
         rcopy(out_at(m_b, v), out_at(m_b, v), rr_send.at[1, v], o_recv, tp=rm).start()
 
-    def attention(nb, diag, tok):
-        per_q = quarter // 128
+    def wide(parts):
+        return jnp.concatenate(parts, axis=1)
+
+    def blocks(ref, first, count):
+        return wide([ref[first + i] for i in range(count)])
+
+    def put_blocks(ref, first, val):
+        for i in range(val.shape[1] // 128):
+            ref[first + i] = val[:, i * 128:(i + 1) * 128]
+
+    def attention(nb, diag, tok, u):
         head_row = lax.broadcasted_iota(jnp.int32, (128, 128), 0) < 64
 
         def project(q):
             for j in range(3):
-                o = jnp.dot(abuf[...], wqkv[q, j], preferred_element_type=jnp.float32)
+                weights = wide([wqkv[q, j * per_q + i] for i in range(per_q)])
+                o = jnp.dot(blocks(abuf, 0, pairs), weights, preferred_element_type=jnp.float32)
                 o = (o + packs[q, 7:8, j * quarter:(j + 1) * quarter]).astype(jnp.bfloat16)
-                if j == 0:
-                    o = o.astype(jnp.float32) * 0.125
-                    for half in range(per_q):
-                        q_t = o[:, half * 128:(half + 1) * 128].T
-                        qaug[q * per_q + half, :128, :128] = jnp.where(head_row, q_t, 0.0).astype(jnp.bfloat16)
-                        qaug[q * per_q + half, :128, 128:] = jnp.where(head_row, 0.0, q_t).astype(jnp.bfloat16)
-                elif j == 1:
-                    kc[q][tok, :] = o
-                else:
-                    vt[q][:, tok] = o.astype(jnp.float32).T.astype(jnp.bfloat16)
+                for i in range(per_q):
+                    part = o[:, i * 128:(i + 1) * 128]
+                    if j == 0:
+                        q_t = (part.astype(jnp.float32) * 0.125).T
+                        qaug[q * per_q + i, 0, :128, :] = jnp.where(head_row, q_t, 0.0).astype(jnp.bfloat16)
+                        qaug[q * per_q + i, 1, :128, :] = jnp.where(head_row, 0.0, q_t).astype(jnp.bfloat16)
+                    elif j == 1:
+                        kc[q][i, tok, :] = part
+                    else:
+                        vt[q][i, u] = part.astype(jnp.float32).T.astype(jnp.bfloat16)
 
         def scores(pair):
-            col = slice(pair % per_q * 128, (pair % per_q + 1) * 128)
             kq = kc[pair // per_q]
+            q_rhs = blocks(qaug.at[pair], 0, 2)
             top = None
             for b in range(nb):
-                keys = jnp.concatenate([kq[b * KBLK:(b + 1) * KBLK, col], kx[b * KBLK:(b + 1) * KBLK, :]], axis=1)
-                s = jnp.dot(keys, qaug[pair], preferred_element_type=jnp.float32)
+                keys = wide([kq[pair % per_q, b * KBLK:(b + 1) * KBLK, :], kx[b * KBLK:(b + 1) * KBLK, :]])
+                s = jnp.dot(keys, q_rhs, preferred_element_type=jnp.float32)
                 if b == nb - 1:
                     s = s + diag
                 sbuf[pair % 2, b] = s
@@ -316,19 +328,18 @@
             return top
 
         def weigh(pair, top):
-            col = slice(pair % per_q * 128, (pair % per_q + 1) * 128)
-            vq = vt[pair // per_q]
+            vq = vt[pair // per_q].at[pair % per_q]
             total = None
             acc = None
             for b in range(nb):
                 e = jnp.exp(sbuf[pair % 2, b] - top)
                 part_sum = jnp.sum(e, axis=0, keepdims=True)
                 total = part_sum if total is None else total + part_sum
-                pv = jnp.dot(vq[col, b * KBLK:(b + 1) * KBLK], e.astype(jnp.bfloat16), preferred_element_type=jnp.float32)
+                pv = jnp.dot(blocks(vq, b * KBLK // UNIT, KBLK // UNIT), e.astype(jnp.bfloat16), preferred_element_type=jnp.float32)
                 acc = pv if acc is None else acc + pv
             acc = acc * (1.0 / total)
             both = jnp.concatenate([acc[:64, :128], acc[64:, 128:]], axis=0)
-            ctx[:, pair * 128:(pair + 1) * 128] = both.T.astype(jnp.bfloat16)
+            ctx[pair] = both.T.astype(jnp.bfloat16)
 
         project(0)
         top = None
@@ -418,27 +429,26 @@
             store_unit(u - hold)
 
         xin = xbuf[u].astype(jnp.float32)
-        abuf[...] = layer_norm(xin, packs[0, 0:1, :], packs[0, 1:2, :])
+        put_blocks(abuf, 0, layer_norm(xin, packs[0, 0:1, :], packs[0, 1:2, :]))
         for nb in range(1, seq // KBLK + 1):
             @pl.when(u // 2 + 1 == nb)
             def _():
-                attention(nb, cmask[u % 2], tok)
-
-        for n in range(model // quarter):
-            cols = slice(n * quarter, (n + 1) * quarter)
-            attn = jnp.dot(ctx[...], wout[:, cols], preferred_element_type=jnp.float32)
+                attention(nb, cmask[u % 2], tok, u)
+
+        for n in range(model // 256):
+            cols = slice(n * 256, (n + 1) * 256)
+            attn = jnp.dot(blocks(ctx, 0, pairs), blocks(wout, 2 * n, 2), preferred_element_type=jnp.float32)
             hbuf[:, cols] = (xbuf[u, :, cols].astype(jnp.float32) + attn + packs[0, 2:3, cols]).astype(jnp.bfloat16)
-        abuf[...] = layer_norm(hbuf[...].astype(jnp.float32), packs[0, 3:4, :], packs[0, 4:5, :])
+        put_blocks(abuf, 0, layer_norm(hbuf[...].astype(jnp.float32), packs[0, 3:4, :], packs[0, 4:5, :]))
         for q in range(tp_n):
-            for n in range(hid_q // quarter):
-                cols = slice(n * quarter, (n + 1) * quarter)
-                up = jnp.dot(abuf[...], wup[q, :, cols], preferred_element_type=jnp.float32)
-                up = up + packs[q, 6:7, cols]
-                ubuf[:, q * hid_q + n * quarter:q * hid_q + (n + 1) * quarter] = gelu(up).astype(jnp.bfloat16)
+            for n in range(hid_q // 256):
+                up = jnp.dot(blocks(abuf, 0, pairs), blocks(wup.at[q], 2 * n, 2), preferred_element_type=jnp.float32)
+                up = up + packs[q, 6:7, n * 256:(n + 1) * 256]
+                put_blocks(ubuf, q * (hid_q // 128) + 2 * n, gelu(up).astype(jnp.bfloat16))
         half_model = model // 2
         for n in range(2):
             cols = slice(n * half_model, (n + 1) * half_model)
-            down = jnp.dot(ubuf[...], wdn[:, cols], preferred_element_type=jnp.float32)
+            down = jnp.dot(blocks(ubuf, 0, ubuf.shape[0]), blocks(wdn, n * (half_model // 128), half_model // 128), preferred_element_type=jnp.float32)
             ybuf[u, :, cols] = (hbuf[:, cols].astype(jnp.float32) + down + packs[0, 5:6, cols]).astype(jnp.bfloat16)
 
             @pl.when(more)
@@ -557,32 +567,32 @@
             in_specs=[anywhere, pl.BlockSpec(memory_space=pltpu.SMEM)] + [anywhere] * 5,
             out_specs=anywhere,
             scratch_shapes=[
-                pltpu.VMEM((tp_size, 3, model_n, quarter), bf16),
-                pltpu.VMEM((tp_size * quarter, model_n), bf16),
-                pltpu.VMEM((tp_size, model_n, hid_q), bf16),
-                pltpu.VMEM((tp_size * hid_q, model_n), bf16),
+                pltpu.VMEM((tp_size, 3 * quarter // 128, model_n, 128), bf16),
+                pltpu.VMEM((model_n // 128, tp_size * quarter, 128), bf16),
+                pltpu.VMEM((tp_size, hid_q // 128, model_n, 128), bf16),
+                pltpu.VMEM((model_n // 128, tp_size * hid_q, 128), bf16),
                 pltpu.VMEM((tp_size,) + pack.shape, f32),
-                pltpu.VMEM((2, 3, model_n // 2, quarter), bf16),
-                pltpu.VMEM((2, quarter // 2, model_n), bf16),
-                pltpu.VMEM((2, model_n // 2, hid_q), bf16),
-                pltpu.VMEM((2, hid_q // 2, model_n), bf16),
-                pltpu.VMEM((3, model_n, quarter), bf16),
-                pltpu.VMEM((quarter, model_n), bf16),
-                pltpu.VMEM((model_n, hid_q), bf16),
-                pltpu.VMEM((hid_q, model_n), bf16),
+                pltpu.VMEM((2, 3 * quarter // 128, model_n // 2, 128), bf16),
+                pltpu.VMEM((2, model_n // 128, quarter // 2, 128), bf16),
+                pltpu.VMEM((2, hid_q // 128, model_n // 2, 128), bf16),
+                pltpu.VMEM((2, model_n // 128, hid_q // 2, 128), bf16),
+                pltpu.VMEM((3 * quarter // 128, model_n, 128), bf16),
+                pltpu.VMEM((model_n // 128, quarter, 128), bf16),
+                pltpu.VMEM((hid_q // 128, model_n, 128), bf16),
+                pltpu.VMEM((model_n // 128, hid_q, 128), bf16),
                 pltpu.VMEM(pack.shape, f32),
                 pltpu.VMEM((units, UNIT, model_n), bf16),
                 pltpu.VMEM((units, UNIT, model_n), bf16),
-                *[pltpu.VMEM((seq_n, quarter), bf16)] * tp_size,
-                *[pltpu.VMEM((quarter, seq_n), bf16)] * tp_size,
+                *[pltpu.VMEM((quarter // 128, seq_n, 128), bf16)] * tp_size,
+                *[pltpu.VMEM((quarter // 128, units, 128, UNIT), bf16)] * tp_size,
                 pltpu.VMEM((seq_n, 128), bf16),
-                pltpu.VMEM((pairs, 256, 256), bf16),
+                pltpu.VMEM((pairs, 2, 256, 128), bf16),
                 pltpu.VMEM((2, KBLK, 256), f32),
                 pltpu.VMEM((2, seq_n // KBLK, KBLK, 256), f32),
+                pltpu.VMEM((model_n // 128, UNIT, 128), bf16),
+                pltpu.VMEM((model_n // 128, UNIT, 128), bf16),
                 pltpu.VMEM((UNIT, model_n), bf16),
-                pltpu.VMEM((UNIT, model_n), bf16),
-                pltpu.VMEM((UNIT, model_n), bf16),
-                pltpu.VMEM((UNIT, tp_size * hid_q), bf16),
+                pltpu.VMEM((tp_size * hid_q // 128, UNIT, 128), bf16),
                 dma((5, 2)), dma((5, 2)), dma((4, 5, 2)), dma((4, 5, 2)), dma((2, 4)), dma((2, 4)), dma((2, 5, 2)), dma((1,)), pltpu.SemaphoreType.REGULAR,
                 *[dma((units,))] * 9,
                 dma((2, units)), dma((2, units)), dma,

time: 299 us -> 296 us (0.990)
  Pallas kernels: 289 us -> 285 us
    pallas_call x1, Pallas kernels: 289 us -> 285 us  [per_device(): pl.pallas_call(functools.partial(kernel, heads_n), out_shape=jax.ShapeDty...]
where the time goes in v9:
time: 296 us; the launch traced here: 295 us
  Pallas kernels  285 us (96%)
  local copies, waits for them, and re-layouts  9.38 us (3%)
    pallas_call x1, Pallas kernels, per_device(): pl.pallas_call(functools.partial(kernel, heads_n), out_shape=jax.ShapeDty...  285 us
    unnamed x1, local copies, waits for them, and re-layouts  7.76 us

profile of v9, /device:TPU:103, one launch (start us, length us, event | category | flops | bytes accessed | tf_op | source)
XLA Modules:
  0.0 295.4 jit_solution(9413322700361143648)
XLA Ops:
  0.0 0.8 reshape.14
  0.8 0.8 concatenate.3
  1.6 0.6 convert_element_type.5.pack_in
  2.2 285.4 %shard_map.136 = bf16[4,1024,1024]{2,1,0:T(8,128)(2,1)} custom-call(bf16[4,1024,1024]{2,1,0:T(8,128)(2,1)} %bitcast.12, s32[4]{0:T(128)} %bitcast.17, bf16[3,1024,256]{2,1,0:T(8,128)(2,1)} %bitcast.15, bf16[256,1024]{1,0:T(8,128)(2,1)} %bitcast.16, bf16[1024,1024]{1,0:T(8,128)(2,1)} %bitcast.13, bf16[1024,1024]{1,0:T(8,128)(2,1)} %bitcast.14, ...), custom_call_target="tpu_custom_call" | custom-call | flops 30000001024 | bytes 40000000 | tf_op jit(solution)/shard_map/pallas_call | solution.py:564
  287.6 7.8 %copy.17 = bf16[1,4,1,1024,1024]{4,3,2,1,0:T(8,128)(2,1)} copy(bf16[1,4,1,1024,1024]{4,3,2,1,0:T(8,128)(2,1)} %bitcast.11) | data formatting | bytes 16777216
  (1 shorter events, 0.0 us)
